TPU v7x, 8 devices: a whole 2x2x1 slice. The times are simulated.
8 devices in a mesh: dp: 1 (over z), tp: 2 (over y), ep: 4 (over x, core).
Axes of the slice: x: 2, y: 2, z: 1, core: 2. Of those that a mesh axis runs over, the one named last changes fastest.
Arguments:
- x: bfloat16 [256, 2048], P(('dp', 'tp', 'ep'))
- route_idx: int32 [256, 8], P(('dp', 'tp', 'ep'))
- gates: float32 [256, 8], P(('dp', 'tp', 'ep'))
- w1: bfloat16 [128, 2048, 768], P('ep', None, 'tp')
- w3: bfloat16 [128, 2048, 768], P('ep', None, 'tp')
- w2: bfloat16 [128, 768, 2048], P('ep', 'tp')
Outputs:
- output: bfloat16 [256, 2048], P(('dp', 'tp', 'ep'))
All inputs are finite; a program needn't handle non-finite values.
Results may differ from a plain program's by a relative error of at most 0.00783045.
Values are sent between devices in bfloat16 or wider.
A program may use at most 1 GiB of HBM per device.

v0:
```python
import jax
import jax.numpy as jnp
from jax import lax
from jax.sharding import PartitionSpec as P


def solution(mesh):
    tp = mesh.shape['tp']
    ep = mesh.shape['ep']
    tok_spec = P(('dp', 'tp', 'ep'), None)

    def local(x, route_idx, gates, w1, w3, w2):
        t_loc, d = x.shape
        top = route_idx.shape[1]
        e_loc = w1.shape[0]
        n_exp = e_loc * ep
        cap = t_loc // 2
        hit = jnp.any(route_idx[:, :, None] == jnp.arange(n_exp, dtype=jnp.int32)[None, None, :], axis=1)
        pos = jnp.cumsum(hit.astype(jnp.int32), axis=0) - 1
        dest = route_idx * cap + jnp.take_along_axis(pos, route_idx, axis=1)
        src = jnp.full((n_exp * cap,), t_loc, jnp.int32).at[dest.reshape(-1)].set(
            jnp.repeat(jnp.arange(t_loc, dtype=jnp.int32), top))
        xp = jnp.concatenate([x, jnp.zeros((1, d), x.dtype)], axis=0)
        send = xp[src].reshape(ep, e_loc * cap, d)
        recv = lax.all_to_all(send, 'ep', 0, 0, tiled=True)
        full = lax.all_gather(recv, 'tp', axis=0, tiled=False)
        rows = full.reshape(tp, ep, e_loc, cap, d).transpose(2, 0, 1, 3, 4).reshape(e_loc, tp * ep * cap, d)
        a = jnp.einsum('erd,edf->erf', rows, w1, preferred_element_type=jnp.float32)
        b = jnp.einsum('erd,edf->erf', rows, w3, preferred_element_type=jnp.float32)
        h = (jax.nn.silu(a) * b).astype(jnp.bfloat16)
        o = jnp.einsum('erf,efd->erd', h, w2, preferred_element_type=jnp.float32)
        o = o.reshape(e_loc, tp, ep, cap, d).transpose(1, 2, 0, 3, 4)
        o = lax.psum_scatter(o, 'tp', scatter_dimension=0, tiled=True)
        o = o.reshape(ep, e_loc * cap, d).astype(jnp.bfloat16)
        back = lax.all_to_all(o, 'ep', 0, 0, tiled=True).reshape(n_exp * cap, d)
        got = back[dest].astype(jnp.float32)
        y = jnp.sum(got * gates[:, :, None], axis=1)
        return y.astype(jnp.bfloat16)

    return jax.shard_map(local, mesh=mesh,
                         in_specs=(tok_spec, tok_spec, tok_spec, P('ep', None, 'tp'), P('ep', None, 'tp'), P('ep', 'tp', None)),
                         out_specs=tok_spec, check_vma=False)
```

profile of v0, /device:TPU:0, one launch (start us, length us, event | category | flops | bytes accessed | tf_op | source)
XLA Modules:
  0.0 926.5 jit_solution(18151288460446247052)
XLA Ops:
  6.5 0.0 all-gather.3.cloned.1.call-start
  6.5 0.8 copy.25
  7.3 0.1 fusion.5
  7.5 0.1 reduce_window_sum.11
  7.5 0.1 reshape.86
  7.6 0.0 copy-start
  7.6 1.9 gather_fusion.2
  9.5 0.1 reshape.89
  9.6 0.6 compare_select_fusion
  10.2 0.1 reshape.63
  10.3 0.1 reshape.96
  10.4 1.4 scatter_custom_fusion
  11.9 0.0 copy-done
  11.9 11.0 %gather_fusion = bf16[2048,2048]{1,0:T(8,128)(2,1)} fusion(bf16[33,2048]{1,0:T(8,128)(2,1)S(1)} %concatenate.3, s32[2048]{0:T(1024)S(1)} %fusion.6), kind=kCustom, calls=%fused_computation | custom fusion | bytes 16785408 | tf_op jit(solution)/shard_map/gather | solution.py:24
  22.9 101.3 %all_to_all.10 = bf16[4,512,2048]{2,1,0:T(8,128)(2,1)} all-to-all(bf16[4,512,2048]{2,1,0:T(8,128)(2,1)} %bitcast.37), channel_id=1, replica_groups=mesh['dp'=1,'tp'=2,'ep'=4] {'ep'}, dimensions={0} | all-to-all | bytes 16777216 | tf_op jit(solution)/shard_map/all_to_all | solution.py:25
  124.2 0.0 all-gather.3.cloned.1.call-update
  124.2 0.0 reduce-scatter.2.cloned.1.call-start
  124.3 197.6 %all-gather.3.cloned.1.call-done = bf16[8,512,2048]{2,1,0:T(8,128)(2,1)} async-done(((bf16[4,512,2048]{2,1,0:T(8,128)(2,1)}), bf16[8,512,2048]{2,1,0:T(8,128)(2,1)}) %all-gather.3.cloned.1.call-update) | async-done | bytes 16777232 | tf_op jit(solution)/shard_map/all_gather | solution.py:26
  321.9 14.1 %copy.30 = bf16[32,2,4,16,2048]{4,3,2,1,0:T(8,128)(2,1)} copy(bf16[32,2,4,16,2048]{4,3,0,2,1:T(8,128)(2,1)} %bitcast.38) | data formatting | bytes 33554432 | tf_op jit(solution)/shard_map/transpose | solution.py:27
  336.0 25.6 %fusion.10 = f32[32,128,384]{2,1,0:T(8,128)} fusion(bf16[32,128,2048]{2,1,0:T(8,128)(2,1)} %bitcast.34, bf16[32,2048,384]{2,1,0:T(8,128)(2,1)} %param.9), kind=kOutput, calls=%fused_computation.25 | convolution fusion | flops 6442450944 | bytes 73400320 | tf_op jit(solution)/shard_map/erd,edf->erf/dot_general | solution.py:28
  361.6 25.6 %multiply_convert_fusion.4 = bf16[32,128,384]{2,1,0:T(8,128)(2,1)S(1)} fusion(f32[32,128,384]{2,1,0:T(8,128)} %fusion.10, bf16[32,128,2048]{2,1,0:T(8,128)(2,1)} %bitcast.35, bf16[32,2048,384]{2,1,0:T(8,128)(2,1)} %param.10), kind=kOutput, calls=%fused_computation.5.clone.clone.1 | convolution fusion | flops 6451888128 | bytes 76546048 | tf_op jit(solution)/shard_map/erd,edf->erf/dot_general | solution.py:29
  387.2 26.9 %fusion = f32[32,128,2048]{2,1,0:T(8,128)} fusion(bf16[32,384,2048]{2,1,0:T(8,128)(2,1)} %param.11, bf16[32,128,384]{2,1,0:T(8,128)(2,1)S(1)} %multiply_convert_fusion.4), kind=kOutput, calls=%fused_computation.6 | convolution fusion | flops 6442450944 | bytes 87031808 | tf_op jit(solution)/shard_map/erf,efd->erd/dot_general | solution.py:31
  414.1 23.1 %copy.34 = f32[32,2,4,16,2048]{4,3,0,2,1:T(8,128)} copy(f32[32,2,4,16,2048]{4,3,2,1,0:T(8,128)} %bitcast.32) | data formatting | bytes 67108864 | tf_op jit(solution)/shard_map/reshape | solution.py:32
  437.2 0.0 reduce-scatter.2.cloned.1.call-update
  437.2 366.3 %reduce-scatter.2.cloned.1.call-done = f32[1,4,32,16,2048]{4,3,2,1,0:T(8,128)} async-done(((f32[2,4,32,16,2048]{4,3,2,1,0:T(8,128)}), f32[1,4,32,16,2048]{4,3,2,1,0:T(8,128)}) %reduce-scatter.2.cloned.1.call-update) | async-done | bytes 16777232 | tf_op jit(solution)/shard_map/reduce_scatter | solution.py:33
  803.5 9.1 convert_element_type.20
  812.6 6.0 all-to-all-start.1
  818.6 0.1 reshape.80
  818.7 0.1 copy.32
  818.8 92.5 %all-to-all-done.1 = bf16[4,512,2048]{2,1,0:T(8,128)(2,1)} async-done(((bf16[4,512,2048]{2,1,0:T(8,128)(2,1)}), bf16[4,512,2048]{2,1,0:T(8,128)(2,1)}, u32[]{:S(2)}, u32[]{:S(2)}) %all-to-all-start.1) | async-done | bytes 8388640 | tf_op jit(solution)/shard_map/all_to_all | solution.py:35
  911.2 6.8 gather_fusion.1
  918.0 1.6 fusion.4
  (12 shorter events, 0.1 us)
Async XLA Ops:
  6.5 315.4 %all-gather.3.cloned.1.call-start = ((), (), s32[]{:S(2)}) async-start(), calls=%async_computation.4 | async-start | bytes 25165824 | tf_op jit(solution)/shard_map/all_gather | solution.py:26
  7.6 4.3 copy-start
  124.2 679.3 %reduce-scatter.2.cloned.1.call-start = ((), (), s32[]{:S(2)}) async-start(), calls=%async_computation.3 | async-start | bytes 50331648 | tf_op jit(solution)/shard_map/reduce_scatter | solution.py:33
  812.6 6.0 copy-start.1
  812.6 6.1 copy-start.2
  812.6 98.7 %all-to-all-start.1 = ((bf16[4,512,2048]{2,1,0:T(8,128)(2,1)}), bf16[4,512,2048]{2,1,0:T(8,128)(2,1)}, u32[]{:S(2)}, u32[]{:S(2)}) async-start(bf16[4,512,2048]{2,1,0:T(8,128)(2,1)} %bitcast.36), calls=%async_computation.2 | async-start | bytes 16777216 | tf_op jit(solution)/shard_map/all_to_all | solution.py:35
Sparse Core Ops, SparseCore 0:
  124.3 197.5 all-gather.2
  437.3 366.0 reduce-scatter.1
where the time goes:
time: 927 us
  waiting for transfers between devices  656 us (71%)
  blocking collectives  101 us (11%)
  matrix products  78.2 us (8%)
  local copies, waits for them, and re-layouts  59.6 us (6%)
  between operations  13.5 us (1%)
  other arithmetic  11.5 us (1%)
    reduce_scatter x1, waiting for transfers between devices, local(): o = lax.psum_scatter(o, 'tp', scatter_dimension=0, tiled=True)  366 us
    all_gather x1, waiting for transfers between devices, local(): full = lax.all_gather(recv, 'tp', axis=0, tiled=False)  198 us
    all_to_all x1, blocking collectives, local(): recv = lax.all_to_all(send, 'ep', 0, 0, tiled=True)  101 us
    all_to_all x1, waiting for transfers between devices, local(): back = lax.all_to_all(o, 'ep', 0, 0, tiled=True).reshape(n_exp * cap, d)  92.5 us
    dot_general x1, matrix products, local(): o = jnp.einsum('erf,efd->erd', h, w2, preferred_element_type=jnp.float32)  26.9 us
    dot_general x1, matrix products, local(): a = jnp.einsum('erd,edf->erf', rows, w1, preferred_element_type=jnp.float32)  25.6 us
    dot_general x1, matrix products, local(): b = jnp.einsum('erd,edf->erf', rows, w3, preferred_element_type=jnp.float32)  25.6 us
    reshape x1, local copies, waits for them, and re-layouts, local(): o = o.reshape(e_loc, tp, ep, cap, d).transpose(1, 2, 0, 3, 4)  23.1 us
  transfers between devices with their start and end apart: 3, of which 3 were waited for; matrix products, arithmetic and copies ran while one was open for 0% of the time, Pallas kernels for 0%

commit v1 on v0

v1 whole, which is shorter than its diff:
```python
import functools

import jax
import jax.numpy as jnp
from jax import lax
from jax.experimental import pallas as pl
from jax.experimental.pallas import tpu as pltpu
from jax.sharding import PartitionSpec as P

MESH = pl.DeviceIdType.MESH
F32 = jnp.float32
BF16 = jnp.bfloat16
BIG = 1e9


def dot(a, b):
    return jnp.dot(a, b, preferred_element_type=F32)


def iota(shape, dim):
    return lax.broadcasted_iota(jnp.int32, shape, dim)


def split3(g):
    g1 = g.astype(BF16)
    r = g - g1.astype(F32)
    g2 = r.astype(BF16)
    g3 = (r - g2.astype(F32)).astype(BF16)
    return g1, g2, g3


def moe_kernel(b, flush, fb, depth, ring, *refs):
    (base_ref, x_ref, route_ref, gates_ref, w1_ref, w3_ref, w2_ref, y_ref, need_ref,
     x_all, r_all, g_all, code, gm, tab_v, tab_s, w1b, w3b, w2b, o_buf, send, recv, y_acc, y_recv,
     gs_sem, gr_sem, tab_sem, w_sem, s_sem, r_sem, fs_sem, fr_sem, ys_sem, yr_sem, fsend) = refs
    tp = lax.axis_index("tp")
    ep = lax.axis_index("ep")
    t_loc, d = x_ref.shape
    n_e = w1_ref.shape[0]
    half = 4 * t_loc
    n_main = n_e * b
    n_rows = n_main + flush
    lag = 4
    peer = {"tp": lax.rem(tp + 1, 2), "ep": ep}

    def weights(e, slot):
        return [pltpu.make_async_copy(w1_ref.at[e], w1b.at[slot], w_sem.at[0, slot]),
                pltpu.make_async_copy(w3_ref.at[e], w3b.at[slot], w_sem.at[1, slot]),
                pltpu.make_async_copy(w2_ref.at[e], w2b.at[slot], w_sem.at[2, slot])]

    for e in range(depth):
        for c in weights(e, e):
            c.start()

    others = [(dt, de) for dt in range(2) for de in range(4) if (dt, de) != (0, 0)]

    def device(dt, de):
        return {"tp": lax.rem(tp + dt, 2), "ep": lax.rem(ep + de, 4)}

    barrier = pltpu.get_barrier_semaphore()
    for dt, de in others:
        pl.semaphore_signal(barrier, inc=1, device_id=device(dt, de), device_id_type=MESH)
    pl.semaphore_wait(barrier, len(others))

    def gather(kind, dt, de):
        src, dst = ((route_ref, r_all), (gates_ref, g_all), (x_ref, x_all))[kind]
        row = pl.multiple_of(dt * half + ep * t_loc, t_loc)
        return pltpu.make_async_remote_copy(
            src_ref=src, dst_ref=dst.at[pl.ds(row, t_loc)], send_sem=gs_sem.at[kind, dt * 4 + de],
            recv_sem=gr_sem.at[kind, dt * 4 + de], device_id=device(dt, de), device_id_type=MESH)

    for kind in range(3):
        for dt, de in others:
            gather(kind, dt, de).start()
    mine = pl.ds(pl.multiple_of(ep * t_loc, t_loc), t_loc)
    r_all[mine, :] = route_ref[...]
    g_all[mine, :] = gates_ref[...]
    x_all[mine, :] = x_ref[...]
    for kind in range(2):
        for dt, de in others:
            gather(kind, dt, de).wait()

    n_tok = 2 * half
    lane = iota((n_tok, 128), 1)
    route = r_all[...]
    gates = g_all[...]
    hit_all = jnp.zeros((n_tok, 128), F32)
    hit = jnp.zeros((n_tok, 128), F32)
    gate = jnp.zeros((half, 128), F32)
    for k in range(route.shape[1]):
        col = route[:, k:k + 1]
        hit_all = jnp.where(col == lane, 1.0, hit_all)
        rel = (col - ep * n_e == lane) & (lane < n_e)
        hit = jnp.where(rel, 1.0, hit)
        gate = jnp.where(rel[:half], gates[:half, k:k + 1], gate)
    cnt_a = jnp.sum(hit_all[:half], axis=0, keepdims=True) - b
    cnt_b = jnp.sum(hit_all[half:], axis=0, keepdims=True) - b
    row16 = iota((16, 128), 0)
    cnt = jnp.where(row16 == 0, cnt_a, jnp.where(row16 == 1, cnt_b, -float(b)))
    k_i, s_i = iota((128, 128), 0), iota((128, 128), 1)
    suffix = ((k_i >= s_i) & (k_i // n_e == s_i // n_e)).astype(BF16)
    need_ref[...] = jnp.max(jnp.max(dot(cnt.astype(BF16), suffix), axis=1, keepdims=True), axis=0, keepdims=True) + jnp.zeros((8, 128), F32)

    t_i, u_i = iota((n_tok, n_tok), 0), iota((n_tok, n_tok), 1)
    before = ((t_i < u_i) & (t_i // half == u_i // half)).astype(BF16)
    hit_t = jnp.transpose(hit)[:n_e, :]
    pos_t = dot(hit_t.astype(BF16), before)
    code[...] = jnp.where(hit_t > 0, pos_t + jnp.where(iota((n_e, n_tok), 1) >= half, float(half // 2), 0.0), -1.0)
    h_i, v_i = iota((half, half), 0), iota((half, half), 1)
    pos = dot((v_i < h_i).astype(BF16), hit[:half].astype(BF16))
    upto = (iota((n_e, n_e), 1) <= iota((n_e, n_e), 0)).astype(BF16)

    k_f = iota((n_e, n_rows), 0).astype(F32)
    i_row = iota((1, n_rows), 1)
    if b:
        step = jnp.where(i_row < n_main, i_row // b, n_e).astype(F32)
        off = jnp.where(i_row < n_main, lax.rem(i_row, b), i_row - n_main).astype(F32)
    else:
        step = jnp.full((1, n_rows), float(n_e), F32)
        off = i_row.astype(F32)

    def table(count, shift):
        c = dot(upto, (count + jnp.zeros((n_e, 128), F32)).astype(BF16))[:, :1]
        total = jnp.max(c, axis=0, keepdims=True)

        def served(m):
            inner = jnp.min(jnp.where(k_f <= m, c + b * (m - k_f), BIG), axis=0, keepdims=True)
            return jnp.minimum(inner, b * (m + 1.0))

        q = served(step - 1.0) + off + base_ref[0].astype(F32)
        end = jnp.where(i_row < n_main, served(step), total)
        valid = q < end
        past = c <= q
        expert = jnp.sum(jnp.where(past, 1.0, 0.0), axis=0, keepdims=True)
        rank = q - jnp.max(jnp.where(past, c, 0.0), axis=0, keepdims=True)
        idx = jnp.where(valid, expert * half + rank + shift, 0.0)
        return idx.astype(jnp.int32), expert, rank, valid

    cnt_a = jnp.sum(hit_t[:, :half], axis=1, keepdims=True)
    cnt_b = jnp.sum(hit_t[:, half:], axis=1, keepdims=True)
    idx_b, _, _, _ = table(cnt_b, float(half // 2))
    idx_a, expert, rank, valid = table(cnt_a, 0.0)
    r8 = iota((8, n_rows), 0)
    tab_v[...] = jnp.where(r8 == 0, idx_b, idx_a)
    to_smem = pltpu.make_async_copy(tab_v, tab_s, tab_sem)
    to_smem.start()
    one = jnp.where((iota((128, n_rows), 0).astype(F32) == expert) & valid, 1.0, 0.0).astype(BF16)
    same = dot(pos.astype(BF16), one) == rank
    for j, g in enumerate(split3(gate)):
        full = jnp.where(same, dot(g, one), 0.0).astype(BF16)
        for m in range(n_rows // 128):
            gm[m, j] = full[:, m * 128:(m + 1) * 128]
    y_acc[...] = jnp.zeros_like(y_acc)
    to_smem.wait()
    for dt, de in others:
        gather(2, dt, de).wait()

    def chunk(e):
        slot = lax.rem(e, ring)
        return pltpu.make_async_remote_copy(
            src_ref=send.at[slot], dst_ref=recv.at[pl.ds(pl.multiple_of(e * b, b), b)], send_sem=s_sem.at[slot],
            recv_sem=r_sem.at[e], device_id=peer, device_id_type=MESH)

    def piece(f):
        return pltpu.make_async_remote_copy(
            src_ref=fsend.at[pl.ds(pl.multiple_of(f * fb, fb), fb)],
            dst_ref=recv.at[pl.ds(pl.multiple_of(n_main + f * fb, fb), fb)], send_sem=fs_sem.at[f],
            recv_sem=fr_sem.at[f], device_id=peer, device_id_type=MESH)


    def partial(way, i):
        return o_buf[pl.ds(jnp.clip(tab_s[way, i], 0, n_e * half - 1), 1), :]

    def add_own(first, rows):
        for r in range(rows):
            i = first + r
            recv[pl.ds(i, 1), :] = recv[pl.ds(i, 1), :] + partial(1, i)

    def combine(m):
        o = recv[pl.ds(pl.multiple_of(m * 128, 128), 128), :].astype(BF16)
        y_acc[...] += dot(gm[m, 0], o) + dot(gm[m, 1], o) + dot(gm[m, 2], o)

    slot_i = iota((half, n_tok), 0).astype(F32)

    @pl.loop(0, n_e)
    def _(e):
        slot = lax.rem(e, depth)
        pick = jnp.where(code[pl.ds(e, 1), :] == slot_i, 1.0, 0.0).astype(BF16)
        xs = dot(pick, x_all[...]).astype(BF16)
        c1, c3, c2 = weights(e, slot)
        c1.wait()
        u = dot(xs, w1b[slot])
        c3.wait()
        v = dot(xs, w3b[slot])
        h = (u * jax.nn.sigmoid(u) * v).astype(BF16)
        c2.wait()
        o_buf[pl.ds(pl.multiple_of(e * half, half), half), :] = dot(h, w2b[slot])

        @pl.when(e + depth < n_e)
        def _():
            for c in weights(e + depth, slot):
                c.start()

        if b:
            @pl.when(e >= ring)
            def _():
                chunk(e - ring).wait_send()

            s = lax.rem(e, ring)
            for r in range(b):
                send[s, r:r + 1, :] = partial(0, e * b + r)
            chunk(e).start()

            @pl.when(e >= lag)
            def _():
                chunk(e - lag).wait_recv()
                add_own((e - lag) * b, b)

            for m in range(n_main // 128 - 1):
                @pl.when(e == (m + 1) * 128 // b - 1 + lag)
                def _():
                    combine(m)

    @pl.loop(0, flush // fb)
    def _(f):
        @pl.loop(0, fb)
        def _(r):
            i = f * fb + r
            fsend[pl.ds(i, 1), :] = partial(0, n_main + i)
        piece(f).start()

    if b:
        @pl.loop(n_e - lag, n_e)
        def _(e):
            chunk(e).wait_recv()
            add_own(e * b, b)
        combine(n_main // 128 - 1)

        @pl.loop(n_e - ring, n_e)
        def _(e):
            chunk(e).wait_send()

    @pl.loop(0, flush // fb)
    def _(f):
        piece(f).wait_recv()

        @pl.loop(0, fb)
        def _(r):
            i = n_main + f * fb + r
            recv[pl.ds(i, 1), :] = recv[pl.ds(i, 1), :] + partial(1, i)

    for m in range(n_main // 128, n_rows // 128):
        combine(m)

    @pl.loop(0, flush // fb)
    def _(f):
        piece(f).wait_send()

    def give(o):
        to = lax.rem(ep + o, 4)
        return pltpu.make_async_remote_copy(
            src_ref=y_acc.at[pl.ds(pl.multiple_of(to * t_loc, t_loc), t_loc)], dst_ref=y_recv.at[3 - o],
            send_sem=ys_sem.at[o - 1], recv_sem=yr_sem.at[3 - o], device_id={"tp": tp, "ep": to}, device_id_type=MESH)

    for o in (2, 1, 3):
        give(o).start()
    y = y_acc[mine, :]
    for o in (1, 3, 2):
        give(o).wait_recv()
        y = y + y_recv[3 - o]
    y_ref[...] = y.astype(y_ref.dtype)
    for o in (1, 2, 3):
        give(o).wait_send()


def moe_call(b, flush, fb, depth, ring, out_dtype, cid, base, x, route, gates, w1, w3, w2):
    t_loc, d = x.shape
    n_e, _, f = w1.shape
    n_rows = n_e * b + flush
    half = 4 * t_loc
    dma = pltpu.SemaphoreType.DMA
    vm = pl.BlockSpec(memory_space=pltpu.VMEM)
    hbm = pl.BlockSpec(memory_space=pl.ANY)
    return pl.pallas_call(
        functools.partial(moe_kernel, b, flush, fb, depth, ring),
        out_shape=(jax.ShapeDtypeStruct((t_loc, d), out_dtype), jax.ShapeDtypeStruct((8, 128), F32)),
        in_specs=[pl.BlockSpec(memory_space=pltpu.SMEM), vm, vm, vm, hbm, hbm, hbm],
        out_specs=(vm, vm),
        scratch_shapes=[
            pltpu.VMEM((2 * half, d), BF16),
            pltpu.VMEM((2 * half, route.shape[1]), jnp.int32),
            pltpu.VMEM((2 * half, route.shape[1]), F32),
            pltpu.VMEM((n_e, 2 * half), F32),
            pltpu.VMEM((n_rows // 128, 3, half, 128), BF16),
            pltpu.VMEM((8, n_rows), jnp.int32),
            pltpu.SMEM((8, n_rows), jnp.int32),
            pltpu.VMEM((depth, d, f), BF16),
            pltpu.VMEM((depth, d, f), BF16),
            pltpu.VMEM((depth, f, d), BF16),
            pltpu.VMEM((n_e * half, d), F32),
            pltpu.VMEM((ring, max(b, 8), d), F32),
            pltpu.VMEM((n_rows, d), F32),
            pltpu.VMEM((half, d), F32),
            pltpu.VMEM((3, t_loc, d), F32),
            dma((3, 8)), dma((3, 8)), dma, dma((3, depth)), dma((ring,)), dma((n_e,)),
            dma((flush // fb,)), dma((flush // fb,)), dma((3,)), dma((3,)),
            pltpu.VMEM((flush, d), F32),
        ],
        compiler_params=pltpu.CompilerParams(collective_id=cid, has_side_effects=True, vmem_limit_bytes=67043328),
    )(base, x, route, gates, w1, w3, w2)


FLUSH = 128


def solution(mesh):
    tok_spec = P(('dp', 'tp', 'ep'), None)

    def local(x, route_idx, gates, w1, w3, w2):
        zero = jnp.zeros((1,), jnp.int32)
        y, need = moe_call(8, FLUSH, 16, 3, 4, BF16, 1, zero, x, route_idx, gates, w1, w3, w2)

        def slow(_):
            part = 256
            total = jnp.zeros(x.shape, F32)

            def one(p, acc):
                base = jnp.full((1,), p * part, jnp.int32)
                return acc + moe_call(0, part, 16, 3, 4, F32, 2, base, x, route_idx, gates, w1, w3, w2)[0]

            return lax.fori_loop(0, 1024 // part, one, total).astype(BF16)

        return lax.cond(need[0, 0] > FLUSH, slow, lambda y: y, y)

    return jax.shard_map(local, mesh=mesh,
                         in_specs=(tok_spec, tok_spec, tok_spec, P('ep', None, 'tp'), P('ep', None, 'tp'), P('ep', 'tp', None)),
                         out_specs=tok_spec, check_vma=False)
```

time: 927 us -> 125 us (0.13)
  waiting for transfers between devices: 656 us -> 0 us
  Pallas kernels: 0 us -> 118 us
  blocking collectives: 101 us -> 0 us
  matrix products: 78.2 us -> 0 us
  local copies, waits for them, and re-layouts: 59.6 us -> 5.49 us
  between operations: 13.5 us -> 0.67 us
  other arithmetic: 11.5 us -> 0 us
    reduce_scatter x1 -> x0, waiting for transfers between devices: 366 us -> none  [local(): o = lax.psum_scatter(o, 'tp', scatter_dimension=0, tiled=True)]
    all_gather x1 -> x0, waiting for transfers between devices: 198 us -> none  [local(): full = lax.all_gather(recv, 'tp', axis=0, tiled=False)]
    pallas_call x0 -> x1, Pallas kernels: none -> 118 us  [moe_call(): pl.pallas_call(functools.partial(moe_kernel, b, flush, fb, depth, ring),...]
    all_to_all x1 -> x0, blocking collectives: 101 us -> none  [local(): recv = lax.all_to_all(send, 'ep', 0, 0, tiled=True)]
    all_to_all x1 -> x0, waiting for transfers between devices: 92.5 us -> none  [local(): back = lax.all_to_all(o, 'ep', 0, 0, tiled=True).reshape(n_exp * cap, d)]
    dot_general x3 -> x0, matrix products: 78.2 us -> none  [the longest x1 26.9 us: local(): o = jnp.einsum('erf,efd->erd', h, w2, preferred_element_type=jnp.float32)]
    reshape x3 -> x0, local copies, waits for them, and re-layouts: 23.2 us -> none  [the longest x1 23.1 us: local(): o = o.reshape(e_loc, tp, ep, cap, d).transpose(1, 2, 0, 3, 4)]
    gather x5 -> x0, local copies, waits for them, and re-layouts: 19.9 us -> none  [the longest x1 11 us: local(): send = xp[src].reshape(ep, e_loc * cap, d)]
  transfers between devices with their start and end apart: 3 -> 0, of which waited for: 3 -> 0; matrix products, arithmetic and copies ran while one was open for 0% -> 0% of each run, Pallas kernels for 0% -> 0%
where the time goes in v1:
time: 125 us
  Pallas kernels  118 us (94%)
  local copies, waits for them, and re-layouts  5.49 us (4%)
    pallas_call x1, Pallas kernels, moe_call(): pl.pallas_call(functools.partial(moe_kernel, b, flush, fb, depth, ring),...  118 us
    unnamed x3, local copies, waits for them, and re-layouts  4.29 us

profile of v1, /device:TPU:0, one launch (start us, length us, event | category | flops | bytes accessed | tf_op | source)
XLA Modules:
  0.0 124.5 jit_solution(8105028741873203632)
XLA Ops:
  0.0 1.4 %copy.9.refs_2_ = s32[32,8]{1,0:T(8,128)} copy(s32[32,8]{0,1:T(8,128)} %param.11) | data formatting | bytes 2048 | tf_op args[1]
  1.4 1.4 %copy.10.refs_3_ = f32[32,8]{1,0:T(8,128)} copy(f32[32,8]{0,1:T(8,128)} %param.12) | data formatting | bytes 2048 | tf_op args[2]
  2.7 118.3 %shard_map.66 = (bf16[32,2048]{1,0:T(8,128)(2,1)}, f32[8,128]{1,0:T(8,128)}) custom-call(s32[1]{0:T(128)} %constant.23.clone.1.refs_0_, bf16[32,2048]{1,0:T(8,128)(2,1)} %refs_1_.1, s32[32,8]{1,0:T(8,128)} %copy.9.refs_2_, f32[32,8]{1,0:T(8,128)} %copy.10.refs_3_, bf16[32,2048,384]{2,1,0:T(8,128)(2,1)} %refs_4_.1, bf16[32,2048,384]{2,1,0:T(8,128)(2,1)} %refs_5_.1, ...), custom_call_target="tpu_custom_call" | custom-call | tf_op jit(solution)/shard_map/pallas_call | solution.py:284
  121.1 1.2 slice.3
  122.9 1.6 %copy.22 = bf16[32,2048]{1,0:T(8,128)(2,1)} copy(bf16[32,2048]{1,0:T(8,128)(2,1)} %get-tuple-element.159) | data formatting | bytes 262144
  (1 shorter events, 0.0 us)

commit v2 on v1

v2 whole, which is shorter than its diff:
```python
import functools

import jax
import jax.numpy as jnp
from jax import lax
from jax.experimental import pallas as pl
from jax.experimental.pallas import tpu as pltpu
from jax.sharding import PartitionSpec as P

MESH = pl.DeviceIdType.MESH
F32 = jnp.float32
BF16 = jnp.bfloat16
BIG = 1e9


def dot(a, b):
    return jnp.dot(a, b, preferred_element_type=F32)


def iota(shape, dim):
    return lax.broadcasted_iota(jnp.int32, shape, dim)


def split3(g):
    g1 = g.astype(BF16)
    r = g - g1.astype(F32)
    g2 = r.astype(BF16)
    g3 = (r - g2.astype(F32)).astype(BF16)
    return g1, g2, g3


def moe_kernel(b, rows_part, cols_part, fb, nb, depth, ring, *refs):
    (base_ref, x_ref, route_ref, gates_ref, w1_ref, w3_ref, w2_ref, y_ref, need_ref,
     x_all, r_all, g_all, before, code, gm, tab_v, tab_s, w1b, w3b, w2b, o_buf, send, fsend, recv, own, y_acc, y_recv,
     gs_sem, gr_sem, xs_sem, xr_sem, tab_sem, w_sem, s_sem, r_sem, fs_sem, fr_sem, cs_sem, cr_sem, ys_sem, yr_sem) = refs
    tp = lax.axis_index("tp")
    ep = lax.axis_index("ep")
    t_loc, d = x_ref.shape
    n_e = w1_ref.shape[0]
    half = 4 * t_loc
    n_tok = 2 * half
    flush = rows_part + cols_part
    n_main = n_e * b
    n_rows = n_main + flush
    lag = 4
    wide = d // nb
    tp_peer = lax.rem(tp + 1, 2)
    ep_x = lax.rem(ep + 2, 4)
    ep_c = ep + 1 - 2 * lax.rem(ep, 2)
    ep_d = lax.rem(ep_c + 2, 4)
    peer = {"tp": tp_peer, "ep": ep}
    dev_x = {"tp": tp, "ep": ep_x}
    dev_c = {"tp": tp, "ep": ep_c}

    def weights(e, slot):
        return [pltpu.make_async_copy(w1_ref.at[e], w1b.at[slot], w_sem.at[0, slot]),
                pltpu.make_async_copy(w3_ref.at[e], w3b.at[slot], w_sem.at[1, slot]),
                pltpu.make_async_copy(w2_ref.at[e], w2b.at[slot], w_sem.at[2, slot])]

    for e in range(depth):
        for c in weights(e, e):
            c.start()

    others = [(dt, de) for dt in range(2) for de in range(4) if (dt, de) != (0, 0)]

    def device(dt, de):
        return {"tp": lax.rem(tp + dt, 2), "ep": lax.rem(ep + de, 4)}

    barrier = pltpu.get_barrier_semaphore()
    for dt, de in others:
        pl.semaphore_signal(barrier, inc=1, device_id=device(dt, de), device_id_type=MESH)

    t_i, u_i = iota((n_tok, n_tok), 0), iota((n_tok, n_tok), 1)
    before[...] = jnp.where((t_i < u_i) & ((t_i < half) == (u_i < half)), 1.0, 0.0).astype(BF16)
    y_acc[...] = jnp.zeros_like(y_acc)
    pl.semaphore_wait(barrier, len(others))

    def gather(kind, dt, de):
        src, dst = ((route_ref, r_all), (gates_ref, g_all))[kind]
        return pltpu.make_async_remote_copy(
            src_ref=src, dst_ref=dst.at[dt * 4 + ep], send_sem=gs_sem.at[kind, dt * 4 + de],
            recv_sem=gr_sem.at[kind, dt * 4 + de], device_id=device(dt, de), device_id_type=MESH)

    def rows_of(first, n):
        return x_all.at[pl.ds(pl.multiple_of(first, 16), n)]

    def x_copy(i, src, dst, to):
        return pltpu.make_async_remote_copy(src_ref=src, dst_ref=dst, send_sem=xs_sem.at[i], recv_sem=xr_sem.at[i],
                                            device_id=to, device_id_type=MESH)

    near, far, h_loc = ep * t_loc, half + ep * t_loc, t_loc // 2
    x_own = [x_copy(0, x_ref, rows_of(near, t_loc), dev_c),
             x_copy(1, x_ref, rows_of(near, t_loc), dev_x),
             x_copy(2, x_ref, rows_of(far, t_loc), peer)]
    nx = ep_x * t_loc
    from_x = [x_copy(4, rows_of(nx, h_loc), rows_of(half + nx, h_loc), peer),
              x_copy(3, rows_of(nx, t_loc), rows_of(nx, t_loc), dev_c)]
    from_y = [x_copy(5, rows_of(far + h_loc, h_loc), rows_of(far + h_loc, h_loc), dev_x),
              x_copy(6, rows_of(far, t_loc), rows_of(far, t_loc), dev_c)]
    from_d = [x_copy(7, rows_of(half + nx, t_loc), rows_of(half + nx, t_loc), dev_c)]

    for kind in range(2):
        for dt, de in others:
            gather(kind, dt, de).start()
    for c in x_own:
        c.start()
    r_all[ep] = route_ref[...]
    g_all[ep] = gates_ref[...]
    x_all[pl.ds(pl.multiple_of(near, t_loc), t_loc), :] = x_ref[...]
    for kind in range(2):
        for dt, de in others:
            gather(kind, dt, de).wait()

    route = jnp.concatenate([r_all[i] for i in range(8)], axis=1)
    gates = jnp.concatenate([g_all[i] for i in range(4)], axis=1)
    n_all = 4 * n_e
    e_all = iota((n_all, n_tok), 0)
    e_loc = iota((n_e, n_tok), 0) + ep * n_e
    hit_all = jnp.zeros((n_all, n_tok), F32)
    hit = jnp.zeros((n_e, n_tok), F32)
    gate = jnp.zeros((n_e, half), F32)
    for k in range(route.shape[0]):
        row = route[k:k + 1, :]
        hit_all = jnp.where(row == e_all, 1.0, hit_all)
        same = row == e_loc
        hit = jnp.where(same, 1.0, hit)
        gate = jnp.where(same[:, :half], gates[k:k + 1, :], gate)
    u2, s2 = iota((n_tok, 128), 0), iota((n_tok, 128), 1)
    side = jnp.where((s2 == 0) & (u2 < half) | (s2 == 1) & (u2 >= half), 1.0, 0.0).astype(BF16)
    k_i, s_i = iota((n_all, n_all), 0), iota((n_all, n_all), 1)
    in_block = functools.reduce(lambda a, c: a | c, [(k_i >= i * n_e) & (k_i < (i + 1) * n_e) & (s_i >= i * n_e) & (s_i < (i + 1) * n_e) for i in range(4)])
    suffix = jnp.where((s_i >= k_i) & in_block, 1.0, 0.0).astype(BF16)
    left = dot(suffix, (dot(hit_all.astype(BF16), side) - b).astype(BF16))
    need_ref[0, 0] = jnp.where(jnp.max(left) > flush, 1, 0)

    hit_b = hit.astype(BF16)
    pos = dot(hit_b, before[...])
    code[...] = jnp.where(hit > 0, pos + jnp.where(iota((n_e, n_tok), 1) >= half, float(half // 2), 0.0), -1.0)
    upto = jnp.where(iota((n_e, n_e), 1) <= iota((n_e, n_e), 0), 1.0, 0.0).astype(BF16)
    cum = dot(upto, dot(hit_b, side).astype(BF16))

    k_f = iota((n_e, n_rows), 0).astype(F32)
    i_f = iota((1, n_rows), 1).astype(F32)
    if b:
        step = jnp.minimum(jnp.floor((i_f + 0.5) * (1.0 / b)), float(n_e))
    else:
        step = jnp.full((1, n_rows), float(n_e), F32)
    off = i_f - step * b

    def table(c, shift):
        total = jnp.max(c, axis=0, keepdims=True)

        def served(m):
            inner = jnp.min(jnp.where(k_f <= m, c + b * (m - k_f), BIG), axis=0, keepdims=True)
            return jnp.minimum(inner, b * (m + 1.0))

        q = served(step - 1.0) + off + base_ref[0].astype(F32)
        end = jnp.where(step < n_e, served(step), total)
        valid = q < end
        past = c <= q
        expert = jnp.sum(jnp.where(past, 1.0, 0.0), axis=0, keepdims=True)
        rank = q - jnp.max(jnp.where(past, c, 0.0), axis=0, keepdims=True)
        idx = jnp.where(valid, expert * half + rank + shift, 0.0)
        return idx.astype(jnp.int32), expert, rank, valid

    idx_b, _, _, _ = table(cum[:, 1:2], float(half // 2))
    idx_a, expert, rank, valid = table(cum[:, 0:1], 0.0)
    r8 = iota((8, n_rows), 0)
    tab_v[...] = jnp.where(r8 == 0, idx_b, idx_a)
    to_smem = pltpu.make_async_copy(tab_v, tab_s, tab_sem)
    to_smem.start()

    for i in (1, 2):
        x_own[i].wait_recv()
        for c in (None, from_x, from_y)[i]:
            c.start()

    def columns(a):
        return jnp.transpose(jnp.concatenate([a, jnp.zeros((128 - n_e, half), F32)], axis=0))

    one = jnp.where((iota((128, n_rows), 0).astype(F32) == expert) & valid, 1.0, 0.0).astype(BF16)
    same = dot(columns(pos[:, :half]).astype(BF16), one) == rank
    for j, g in enumerate(split3(columns(gate))):
        full = jnp.where(same, dot(g, one), 0.0).astype(BF16)
        for m in range(n_rows // 128):
            gm[m, j] = full[:, m * 128:(m + 1) * 128]

    from_x[0].wait_recv()
    from_y[0].wait_recv()
    from_d[0].start()
    to_smem.wait()
    x_own[0].wait_recv()
    from_x[1].wait_recv()
    from_y[1].wait_recv()
    from_d[0].wait_recv()

    def chunk(e):
        slot = lax.rem(e, ring)
        return pltpu.make_async_remote_copy(
            src_ref=send.at[slot], dst_ref=recv.at[pl.ds(pl.multiple_of(e * b, b), b)], send_sem=s_sem.at[slot],
            recv_sem=r_sem.at[e], device_id=peer, device_id_type=MESH)

    def piece(f):
        return pltpu.make_async_remote_copy(
            src_ref=fsend.at[pl.ds(pl.multiple_of(f * fb, fb), fb)],
            dst_ref=recv.at[pl.ds(pl.multiple_of(n_main + f * fb, fb), fb)], send_sem=fs_sem.at[f],
            recv_sem=fr_sem.at[f], device_id=peer, device_id_type=MESH)

    def col_piece(n):
        cols = pl.ds(n * wide, wide)
        return pltpu.make_async_remote_copy(
            src_ref=fsend.at[pl.ds(rows_part, cols_part), cols],
            dst_ref=recv.at[pl.ds(n_main + rows_part, cols_part), cols], send_sem=cs_sem.at[n],
            recv_sem=cr_sem.at[n], device_id=peer, device_id_type=MESH)

    def partial(way, i):
        return o_buf[pl.ds(jnp.clip(tab_s[way, i], 0, n_e * half - 1), 1), :]

    def pack_send(e):
        s = lax.rem(e, ring)
        for r in range(b):
            send[s, r:r + 1, :] = partial(0, e * b + r)

    def pack_own(e):
        first = pl.multiple_of(lax.rem(e * b, 128), b)
        for r in range(b):
            own[pl.ds(first + r, 1), :] = partial(1, e * b + r)

    def combine(m, cols):
        o = (recv[m * 128:(m + 1) * 128, cols] + own[:, cols]).astype(BF16)
        y_acc[:, cols] += dot(gm[m, 0], o) + dot(gm[m, 1], o) + dot(gm[m, 2], o)

    def combine_main(m):
        @pl.loop(m * (128 // b), (m + 1) * (128 // b))
        def _(e):
            chunk(e).wait_recv()
        combine(m, slice(None))

    slot_i = iota((half, n_tok), 0).astype(F32)

    @pl.loop(0, n_e)
    def _(e):
        slot = lax.rem(e, depth)
        if b:
            @pl.when(e > ring)
            def _():
                chunk(e - 1 - ring).wait_send()
        for c in weights(e, slot):
            c.wait()
        if b:
            pack_send(jnp.maximum(e - 1, 0))
            pack_own(jnp.maximum(e - lag, 0))
        pick = jnp.where(code[pl.ds(e, 1), :] == slot_i, 1.0, 0.0).astype(BF16)
        xs = dot(pick, x_all[...]).astype(BF16)
        u = dot(xs, w1b[slot])
        v = dot(xs, w3b[slot])
        h = (u * jax.nn.sigmoid(u) * v).astype(BF16)
        o_buf[pl.ds(pl.multiple_of(e * half, half), half), :] = dot(h, w2b[slot])
        if b:
            @pl.when(e >= 1)
            def _():
                chunk(e - 1).start()

        @pl.when(e + depth < n_e)
        def _():
            for c in weights(e + depth, slot):
                c.start()

        if b:
            for m in range(n_main // 128 - 1):
                @pl.when(e == (m + 1) * 128 // b - 1 + lag)
                def _():
                    combine_main(m)

    if b:
        chunk(n_e - 1 - ring).wait_send()
        pack_send(n_e - 1)
        chunk(n_e - 1).start()

    @pl.loop(0, rows_part // fb)
    def _(f):
        for r in range(fb):
            fsend[pl.ds(pl.multiple_of(f * fb, fb) + r, 1), :] = partial(0, n_main + f * fb + r)
        piece(f).start()

    @pl.loop(0, cols_part // 8)
    def _(f):
        for r in range(8):
            i = rows_part + f * 8 + r
            fsend[pl.ds(i, 1), :] = partial(0, n_main + i)
    for n in range(nb):
        col_piece(n).start()

    if b:
        @pl.loop(n_e - lag, n_e)
        def _(e):
            pack_own(e)
        combine_main(n_main // 128 - 1)

        @pl.loop(n_e - ring, n_e)
        def _(e):
            chunk(e).wait_send()

    def give(o, n):
        to = lax.rem(ep + o, 4)
        cols = pl.ds(n * wide, wide)
        return pltpu.make_async_remote_copy(
            src_ref=y_acc.at[pl.ds(pl.multiple_of(to * t_loc, t_loc), t_loc), cols], dst_ref=y_recv.at[3 - o, :, cols],
            send_sem=ys_sem.at[o - 1, n], recv_sem=yr_sem.at[3 - o, n], device_id={"tp": tp, "ep": to}, device_id_type=MESH)

    last = n_rows // 128 - 1
    for m in range(n_main // 128, last + 1):
        @pl.loop(0, 16)
        def _(f):
            for r in range(8):
                own[pl.ds(pl.multiple_of(f * 8, 8) + r, 1), :] = partial(1, m * 128 + f * 8 + r)
        if m < last:
            for f in range(128 // fb):
                piece((m * 128 - n_main) // fb + f).wait_recv()
            combine(m, slice(None))
    for f in range((last * 128 - n_main) // fb, rows_part // fb):
        piece(f).wait_recv()
    for n in range(nb):
        col_piece(n).wait_recv()
        combine(last, slice(n * wide, (n + 1) * wide))
        for o in (2, 1, 3):
            give(o, n).start()
    mine = pl.ds(pl.multiple_of(near, t_loc), t_loc)
    for n in range(nb):
        cols = slice(n * wide, (n + 1) * wide)
        y = y_acc[mine, cols]
        for o in (1, 3, 2):
            give(o, n).wait_recv()
            y = y + y_recv[3 - o, :, cols]
        y_ref[:, cols] = y.astype(y_ref.dtype)

    for f in range(rows_part // fb):
        piece(f).wait_send()
    for n in range(nb):
        col_piece(n).wait_send()
        for o in (1, 2, 3):
            give(o, n).wait_send()
    for c in x_own + from_x + from_y + from_d:
        c.wait_send()


def moe_call(b, rows_part, cols_part, fb, nb, depth, ring, out_dtype, cid, base, x, route, gates, w1, w3, w2):
    t_loc, d = x.shape
    n_e, _, f = w1.shape
    n_rows = n_e * b + rows_part + cols_part
    half = 4 * t_loc
    dma = pltpu.SemaphoreType.DMA
    vm = pl.BlockSpec(memory_space=pltpu.VMEM)
    sm = pl.BlockSpec(memory_space=pltpu.SMEM)
    hbm = pl.BlockSpec(memory_space=pl.ANY)
    return pl.pallas_call(
        functools.partial(moe_kernel, b, rows_part, cols_part, fb, nb, depth, ring),
        out_shape=(jax.ShapeDtypeStruct((t_loc, d), out_dtype), jax.ShapeDtypeStruct((1, 1), jnp.int32)),
        in_specs=[sm, vm, vm, vm, hbm, hbm, hbm],
        out_specs=(vm, sm),
        scratch_shapes=[
            pltpu.VMEM((2 * half, d), BF16),
            pltpu.VMEM((8,) + route.shape, jnp.int32),
            pltpu.VMEM((8,) + route.shape, F32),
            pltpu.VMEM((2 * half, 2 * half), BF16),
            pltpu.VMEM((n_e, 2 * half), F32),
            pltpu.VMEM((n_rows // 128, 3, half, 128), BF16),
            pltpu.VMEM((8, n_rows), jnp.int32),
            pltpu.SMEM((8, n_rows), jnp.int32),
            pltpu.VMEM((depth, d, f), BF16),
            pltpu.VMEM((depth, d, f), BF16),
            pltpu.VMEM((depth, f, d), BF16),
            pltpu.VMEM((n_e * half, d), F32),
            pltpu.VMEM((ring, max(b, 8), d), F32),
            pltpu.VMEM((rows_part + cols_part, d), F32),
            pltpu.VMEM((n_rows, d), F32),
            pltpu.VMEM((128, d), F32),
            pltpu.VMEM((half, d), F32),
            pltpu.VMEM((3, t_loc, d), F32),
            dma((2, 8)), dma((2, 8)), dma((8,)), dma((8,)), dma, dma((3, depth)), dma((ring,)), dma((n_e,)),
            dma((rows_part // fb,)), dma((rows_part // fb,)), dma((nb,)), dma((nb,)), dma((3, nb)), dma((3, nb)),
        ],
        compiler_params=pltpu.CompilerParams(collective_id=cid, has_side_effects=True, vmem_limit_bytes=67043328),
    )(base, x, route, gates, w1, w3, w2)


def solution(mesh):
    tok_spec = P(('dp', 'tp', 'ep'), None)

    def local(x, route_idx, gates, w1, w3, w2):
        zero = jnp.zeros((1,), jnp.int32)
        rt, gt = route_idx.T, gates.T
        y, need = moe_call(8, 64, 64, 16, 4, 3, 4, BF16, 1, zero, x, rt, gt, w1, w3, w2)

        def slow(_):
            part = 256

            def one(p, acc):
                base = jnp.full((1,), p * part, jnp.int32)
                return acc + moe_call(0, part - 64, 64, 16, 4, 3, 4, F32, 2, base, x, rt, gt, w1, w3, w2)[0]

            return lax.fori_loop(0, 1024 // part, one, jnp.zeros(x.shape, F32)).astype(BF16)

        return lax.cond(need[0, 0] > 0, slow, lambda y: y, y)

    return jax.shard_map(local, mesh=mesh,
                         in_specs=(tok_spec, tok_spec, tok_spec, P('ep', None, 'tp'), P('ep', None, 'tp'), P('ep', 'tp', None)),
                         out_specs=tok_spec, check_vma=False)
```

time: 125 us -> 96.2 us (0.77)
  Pallas kernels: 118 us -> 93.8 us
  local copies, waits for them, and re-layouts: 5.49 us -> 1.57 us
    pallas_call x1, Pallas kernels: 118 us -> 93.8 us  [moe_call(): pl.pallas_call(functools.partial(moe_kernel, b, rows_part, cols_part, fb,...]
    unnamed x3 -> x1, local copies, waits for them, and re-layouts: 4.29 us -> 1.57 us
where the time goes in v2:
time: 96.2 us; the launch traced here: 96.1 us
  Pallas kernels  93.8 us (98%)
  local copies, waits for them, and re-layouts  1.57 us (2%)
    pallas_call x1, Pallas kernels, moe_call(): pl.pallas_call(functools.partial(moe_kernel, b, rows_part, cols_part, fb,...  93.8 us

profile of v2, /device:TPU:0, one launch (start us, length us, event | category | flops | bytes accessed | tf_op | source)
XLA Modules:
  0.0 96.1 jit_solution(11956887047963174684)
XLA Ops:
  0.0 93.8 %shard_map.66 = (bf16[32,2048]{1,0:T(8,128)(2,1)}, s32[1,1]{1,0:T(1,128)}) custom-call(s32[1]{0:T(128)} %constant.23.clone.1.refs_0_, bf16[32,2048]{1,0:T(8,128)(2,1)} %refs_1_.1, s32[8,32]{1,0:T(8,128)} %bitcast.6, f32[8,32]{1,0:T(8,128)} %bitcast.8, bf16[32,2048,384]{2,1,0:T(8,128)(2,1)} %refs_4_.1, bf16[32,2048,384]{2,1,0:T(8,128)(2,1)} %refs_5_.1, ...), custom_call_target="tpu_custom_call" | custom-call | tf_op jit(solution)/shard_map/pallas_call | solution.py:356
  94.5 1.6 %copy.18 = bf16[32,2048]{1,0:T(8,128)(2,1)} copy(bf16[32,2048]{1,0:T(8,128)(2,1)} %get-tuple-element.159) | data formatting | bytes 262144
  (1 shorter events, 0.0 us)

commit v3 on v2

v3 whole, which is shorter than its diff:
```python
import functools

import jax
import jax.numpy as jnp
from jax import lax
from jax.experimental import pallas as pl
from jax.experimental.pallas import tpu as pltpu
from jax.sharding import PartitionSpec as P

MESH = pl.DeviceIdType.MESH
F32 = jnp.float32
BF16 = jnp.bfloat16
BIG = 1e9


def dot(a, b):
    return jnp.dot(a, b, preferred_element_type=F32)


def iota(shape, dim):
    return lax.broadcasted_iota(jnp.int32, shape, dim)


def split3(g):
    g1 = g.astype(BF16)
    r = g - g1.astype(F32)
    g2 = r.astype(BF16)
    g3 = (r - g2.astype(F32)).astype(BF16)
    return g1, g2, g3


def moe_kernel(b, rows_part, cols_part, fb, nb, depth, ring, *refs):
    (base_ref, x_ref, route_ref, gates_ref, w1_ref, w3_ref, w2_ref, y_ref, need_ref,
     x_all, r_all, g_all, before, code, gm, gf, tab_v, tab_s, w1b, w3b, w2b, o_buf, send, recv, own, y_acc, y_recv,
     cand, swap, f_send, f_recv,
     gs_sem, gr_sem, xs_sem, xr_sem, tab_sem, w_sem, s_sem, r_sem, ds_sem, dr_sem, fs_sem, fr_sem, cs_sem, cr_sem,
     ys_sem, yr_sem) = refs
    tp = lax.axis_index("tp")
    ep = lax.axis_index("ep")
    t_loc, d = x_ref.shape
    n_e = w1_ref.shape[0]
    half = 4 * t_loc
    n_tok = 2 * half
    flush = rows_part + cols_part
    n_main = n_e * b
    lag = 4
    hw = d // 2
    wide = hw // nb
    core = lax.rem(ep, 2)
    tp_peer = lax.rem(tp + 1, 2)
    ep_x = lax.rem(ep + 2, 4)
    ep_c = ep + 1 - 2 * lax.rem(ep, 2)
    ep_d = lax.rem(ep_c + 2, 4)
    peer = {"tp": tp_peer, "ep": ep}
    dev_x = {"tp": tp, "ep": ep_x}
    dev_c = {"tp": tp, "ep": ep_c}

    def weights(e, slot):
        return [pltpu.make_async_copy(w1_ref.at[e], w1b.at[slot], w_sem.at[0, slot]),
                pltpu.make_async_copy(w3_ref.at[e], w3b.at[slot], w_sem.at[1, slot]),
                pltpu.make_async_copy(w2_ref.at[e], w2b.at[slot], w_sem.at[2, slot])]

    for e in range(depth):
        for c in weights(e, e):
            c.start()

    others = [(dt, de) for dt in range(2) for de in range(4) if (dt, de) != (0, 0)]

    def device(dt, de):
        return {"tp": lax.rem(tp + dt, 2), "ep": lax.rem(ep + de, 4)}

    barrier = pltpu.get_barrier_semaphore()
    for dt, de in others:
        pl.semaphore_signal(barrier, inc=1, device_id=device(dt, de), device_id_type=MESH)

    t_i, u_i = iota((n_tok, n_tok), 0), iota((n_tok, n_tok), 1)
    before[...] = jnp.where((t_i < u_i) & ((t_i < half) == (u_i < half)), 1.0, 0.0).astype(BF16)
    y_acc[...] = jnp.zeros_like(y_acc)
    o_buf[n_e * half:, :] = jnp.zeros((8, d), F32)
    pl.semaphore_wait(barrier, len(others))

    def gather(kind, dt, de):
        src, dst = ((route_ref, r_all), (gates_ref, g_all))[kind]
        return pltpu.make_async_remote_copy(
            src_ref=src, dst_ref=dst.at[dt * 4 + ep], send_sem=gs_sem.at[kind, dt * 4 + de],
            recv_sem=gr_sem.at[kind, dt * 4 + de], device_id=device(dt, de), device_id_type=MESH)

    def rows_of(first, n):
        return x_all.at[pl.ds(pl.multiple_of(first, 16), n)]

    def x_copy(i, src, dst, to):
        return pltpu.make_async_remote_copy(src_ref=src, dst_ref=dst, send_sem=xs_sem.at[i], recv_sem=xr_sem.at[i],
                                            device_id=to, device_id_type=MESH)

    near, far, h_loc = ep * t_loc, half + ep * t_loc, t_loc // 2
    nx = ep_x * t_loc
    x_own = [x_copy(0, x_ref.at[pl.ds(0, h_loc)], rows_of(near, h_loc), dev_x),
             x_copy(1, x_ref.at[pl.ds(h_loc, h_loc)], rows_of(far + h_loc, h_loc), peer),
             x_copy(2, x_ref.at[pl.ds(h_loc, h_loc)], rows_of(near + h_loc, h_loc), dev_x),
             x_copy(3, x_ref.at[pl.ds(0, h_loc)], rows_of(far, h_loc), peer),
             x_copy(4, x_ref, rows_of(near, t_loc), dev_c)]

    def passed(i, row, n, to):
        return x_copy(i, rows_of(row, n), rows_of(row, n), to)

    to_y = x_copy(5, rows_of(nx, h_loc), rows_of(half + nx, h_loc), peer)
    to_x = passed(6, far + h_loc, h_loc, dev_x)
    to_c = [passed(7, nx, t_loc, dev_c), passed(8, far, t_loc, dev_c),
            passed(9, half + nx, h_loc, dev_c), passed(10, half + nx + h_loc, h_loc, dev_c)]

    for kind in range(2):
        for dt, de in others:
            gather(kind, dt, de).start()
    for c in x_own:
        c.start()
    r_all[ep] = route_ref[...]
    g_all[ep] = gates_ref[...]
    x_all[pl.ds(pl.multiple_of(near, t_loc), t_loc), :] = x_ref[...]
    for kind in range(2):
        for dt, de in others:
            gather(kind, dt, de).wait()

    route = jnp.concatenate([r_all[i] for i in range(8)], axis=1)
    gates = jnp.concatenate([g_all[i] for i in range(4)], axis=1)
    n_all = 4 * n_e
    e_all = iota((n_all, n_tok), 0)
    e_two = iota((2 * n_e, n_tok), 0)
    e_two = jnp.where(e_two < n_e, e_two + ep * n_e, e_two + (ep_c - 1) * n_e)
    hit_all = jnp.zeros((n_all, n_tok), F32)
    hit = jnp.zeros((2 * n_e, n_tok), F32)
    gate = jnp.zeros((2 * n_e, half), F32)
    for k in range(route.shape[0]):
        row = route[k:k + 1, :]
        hit_all = jnp.where(row == e_all, 1.0, hit_all)
        same = row == e_two
        hit = jnp.where(same, 1.0, hit)
        gate = jnp.where(same[:, :half], gates[k:k + 1, :], gate)
    u2, s2 = iota((n_tok, 128), 0), iota((n_tok, 128), 1)
    side = jnp.where((s2 == 0) & (u2 < half) | (s2 == 1) & (u2 >= half), 1.0, 0.0).astype(BF16)
    k_i, s_i = iota((n_all, n_all), 0), iota((n_all, n_all), 1)
    in_block = functools.reduce(lambda a, c: a | c, [(k_i >= i * n_e) & (k_i < (i + 1) * n_e) & (s_i >= i * n_e) & (s_i < (i + 1) * n_e) for i in range(4)])
    suffix = jnp.where((s_i >= k_i) & in_block, 1.0, 0.0).astype(BF16)
    left = dot(suffix, (dot(hit_all.astype(BF16), side) - b).astype(BF16))
    left = [jnp.maximum(jnp.max(left[i * n_e:(i + 1) * n_e], axis=0, keepdims=True), 0.0) for i in range(4)]
    need_ref[0, 0] = jnp.where(jnp.max(jnp.maximum(left[0] + left[1], left[2] + left[3])) > flush, 1, 0)

    hit_b = hit.astype(BF16)
    pos = dot(hit_b, before[...])
    code[...] = jnp.where(hit > 0, pos + jnp.where(iota((2 * n_e, n_tok), 1) >= half, float(half // 2), 0.0), -1.0)[:n_e]
    two = 2 * n_e
    up_i, up_j = iota((two, two), 0), iota((two, two), 1)
    upto = jnp.where((up_j <= up_i) & ((up_j < n_e) == (up_i < n_e)), 1.0, 0.0).astype(BF16)
    cum = dot(upto, dot(hit_b, side).astype(BF16))

    def served(c, m, k_f):
        inner = jnp.min(jnp.where(k_f <= m, c + b * (m - k_f), BIG), axis=0, keepdims=True)
        return jnp.minimum(inner, b * (m + 1.0))

    def locate(c, q, valid, shift):
        past = c <= q
        expert = jnp.sum(jnp.where(past, 1.0, 0.0), axis=0, keepdims=True)
        rank = q - jnp.max(jnp.where(past, c, 0.0), axis=0, keepdims=True)
        idx = jnp.where(valid, expert * half + rank + shift, float(n_e * half))
        return idx.astype(jnp.int32), expert, rank

    def main_table(way, shift):
        c = cum[:n_e, way:way + 1]
        k_f = iota((n_e, n_main), 0).astype(F32)
        i_f = iota((1, n_main), 1).astype(F32)
        step = jnp.floor((i_f + 0.5) * (1.0 / b))
        q = served(c, step - 1.0, k_f) + (i_f - step * b)
        valid = q < served(c, step, k_f)
        return locate(c, q, valid, shift) + (valid,)

    def flush_table(way, shift):
        k_f = iota((n_e, 256), 0).astype(F32)
        i_f = iota((1, 256), 1).astype(F32) + base_ref[0].astype(F32)
        both = []
        for c in (cum[:n_e, way:way + 1], cum[n_e:, way:way + 1]):
            done = served(c, float(n_e - 1), k_f)
            both.append((c, done, jnp.max(c, axis=0, keepdims=True) - done))
        second = core.astype(F32)
        out = []
        for (c, done, rest), first in zip(both, (second * both[1][2], (1.0 - second) * both[0][2])):
            i = i_f - first
            valid = (i >= 0) & (i < rest)
            out.append(locate(c, done + i, valid, shift) + (valid,))
        return out

    def one_hot(expert, valid, n):
        return jnp.where((iota((n, expert.shape[1]), 0).astype(F32) == expert) & valid, 1.0, 0.0)

    b_own, _ = flush_table(1, float(half // 2))
    a_own, a_par = flush_table(0, 0.0)
    picks = [(b_own[0], a_own[0], jnp.concatenate([one_hot(a_own[1], a_own[3], n_e), one_hot(a_par[1], a_par[3], n_e),
                                                   jnp.zeros((128 - two, 256), F32)], axis=0),
              jnp.where(a_own[3], a_own[2], a_par[2]))]
    if b:
        m_b, m_a = main_table(1, float(half // 2)), main_table(0, 0.0)
        picks.insert(0, (m_b[0], m_a[0], one_hot(m_a[1], m_a[3], 128), m_a[2]))
    idx_b, idx_a, one, rank = [jnp.concatenate(p, axis=1) for p in zip(*picks)]
    tab_v[...] = jnp.where(iota(tab_v.shape, 0) == 0, idx_b, idx_a)
    to_smem = pltpu.make_async_copy(tab_v, tab_s, tab_sem)
    to_smem.start()

    x_own[0].wait_recv()
    to_y.start()
    x_own[1].wait_recv()
    to_x.start()
    x_own[2].wait_recv()
    to_c[0].start()
    x_own[3].wait_recv()
    to_c[1].start()

    def columns(a):
        return jnp.transpose(jnp.concatenate([a, jnp.zeros((128 - two, half), F32)], axis=0))

    one = one.astype(BF16)
    same = dot(columns(pos[:, :half]).astype(BF16), one) == rank
    for j, g in enumerate(split3(columns(gate))):
        full = jnp.where(same, dot(g, one), 0.0).astype(BF16)
        for m in range(n_main // 128):
            gm[m, j] = full[:, m * 128:(m + 1) * 128]
        gf[j] = full[:, n_main:]

    to_y.wait_recv()
    to_c[2].start()
    to_x.wait_recv()
    to_c[3].start()
    to_smem.wait()
    x_own[4].wait_recv()
    for c in to_c:
        c.wait_recv()

    def chunk(e):
        slot = lax.rem(e, ring)
        return pltpu.make_async_remote_copy(
            src_ref=send.at[slot], dst_ref=recv.at[pl.ds(pl.multiple_of(e * b, b), b)], send_sem=s_sem.at[slot],
            recv_sem=r_sem.at[e], device_id=peer, device_id_type=MESH)

    def swapped(way, f):
        rows = pl.ds(f * fb, fb) if f < rows_part // fb else pl.ds(rows_part, cols_part)
        return pltpu.make_async_remote_copy(
            src_ref=cand.at[way, 1 - core, rows], dst_ref=swap.at[way, rows], send_sem=ds_sem.at[way, f],
            recv_sem=dr_sem.at[way, f], device_id=dev_c, device_id_type=MESH)

    def piece(f):
        rows = pl.ds(f * fb, fb)
        return pltpu.make_async_remote_copy(src_ref=f_send.at[rows], dst_ref=f_recv.at[rows], send_sem=fs_sem.at[f],
                                            recv_sem=fr_sem.at[f], device_id=peer, device_id_type=MESH)

    def col_piece(n):
        at = (pl.ds(rows_part, cols_part), pl.ds(n * wide, wide))
        return pltpu.make_async_remote_copy(src_ref=f_send.at[at], dst_ref=f_recv.at[at], send_sem=cs_sem.at[n],
                                            recv_sem=cr_sem.at[n], device_id=peer, device_id_type=MESH)

    def partial(way, i):
        return o_buf[pl.ds(jnp.clip(tab_s[way, i], 0, n_e * half), 1), :]

    def pack_send(e):
        s = lax.rem(e, ring)
        for r in range(b):
            send[s, r:r + 1, :] = partial(0, e * b + r)

    def pack_own(e):
        first = pl.multiple_of(lax.rem(e * b, 128), b)
        for r in range(b):
            own[pl.ds(first + r, 1), :] = partial(1, e * b + r)

    def combine_main(m):
        @pl.loop(m * (128 // b), (m + 1) * (128 // b))
        def _(e):
            chunk(e).wait_recv()
        for h in range(2):
            cols = slice(h * hw, (h + 1) * hw)
            o = (recv[m * 128:(m + 1) * 128, cols] + own[:, cols]).astype(BF16)
            y_acc[h] += dot(gm[m, 0], o) + dot(gm[m, 1], o) + dot(gm[m, 2], o)

    def combine_flush(rows, cols):
        o = (f_recv[rows, cols] + (cand[0, core, rows, cols] + swap[0, rows, cols])).astype(BF16)
        y_acc[core, :, cols] += dot(gf[0, :, rows], o) + dot(gf[1, :, rows], o) + dot(gf[2, :, rows], o)

    slot_i = iota((half, n_tok), 0).astype(F32)

    @pl.loop(0, n_e)
    def _(e):
        slot = lax.rem(e, depth)
        if b:
            @pl.when(e > ring)
            def _():
                chunk(e - 1 - ring).wait_send()

            @pl.when(e >= 1)
            def _():
                pack_send(e - 1)
                chunk(e - 1).start()
        for c in weights(e, slot):
            c.wait()
        if b:
            pack_own(jnp.maximum(e - lag, 0))
        pick = jnp.where(code[pl.ds(e, 1), :] == slot_i, 1.0, 0.0).astype(BF16)
        xs = dot(pick, x_all[...]).astype(BF16)
        u = dot(xs, w1b[slot])
        v = dot(xs, w3b[slot])
        h = (u * jax.nn.sigmoid(u) * v).astype(BF16)
        o_buf[pl.ds(pl.multiple_of(e * half, half), half), :] = dot(h, w2b[slot])

        @pl.when(e + depth < n_e)
        def _():
            for c in weights(e + depth, slot):
                c.start()

        if b:
            for m in range(n_main // 128 - 1):
                @pl.when(e == (m + 1) * 128 // b - 1 + lag)
                def _():
                    combine_main(m)

    if b:
        chunk(n_e - 1 - ring).wait_send()
        pack_send(n_e - 1)
        chunk(n_e - 1).start()

    n_piece = rows_part // fb + 1

    def pack_cand(way, f):
        first, n = (f * fb, fb) if f < n_piece - 1 else (rows_part, cols_part)

        @pl.loop(0, n // 8)
        def _(g):
            for r in range(8):
                i = first + g * 8 + r
                row = partial(1 - way, n_main + i)
                cand[way, 0, pl.ds(i, 1), :] = row[:, :hw]
                cand[way, 1, pl.ds(i, 1), :] = row[:, hw:]
        swapped(way, f).start()

    def join_send(f):
        swapped(1, f).wait_recv()
        rows = slice(f * fb, (f + 1) * fb) if f < n_piece - 1 else slice(rows_part, flush)
        f_send[rows, :] = cand[1, core, rows, :] + swap[1, rows, :]
        if f < n_piece - 1:
            piece(f).start()
        else:
            for n in range(nb):
                col_piece(n).start()

    def give(o, n):
        to = lax.rem(ep + o, 4)
        h, cols = (core, pl.ds(n * wide, wide)) if n < nb else (1 - core, pl.ds(0, hw))
        return pltpu.make_async_remote_copy(
            src_ref=y_acc.at[h, pl.ds(pl.multiple_of(to * t_loc, t_loc), t_loc), cols], dst_ref=y_recv.at[3 - o, h, :, cols],
            send_sem=ys_sem.at[o - 1, n], recv_sem=yr_sem.at[3 - o, n], device_id={"tp": tp, "ep": to}, device_id_type=MESH)

    for f in range(2):
        pack_cand(1, f)
    for f in range(n_piece):
        join_send(f)
        if f + 2 < n_piece:
            pack_cand(1, f + 2)
    if b:
        @pl.loop(n_e - lag, n_e)
        def _(e):
            pack_own(e)
        combine_main(n_main // 128 - 1)
    for o in (2, 1, 3):
        give(o, nb).start()
    for f in range(n_piece):
        pack_cand(0, f)
    for f in range(n_piece):
        swapped(0, f).wait_recv()
    for f in range(n_piece - 1):
        piece(f).wait_recv()
    combine_flush(slice(0, rows_part), slice(0, hw))
    for n in range(nb):
        col_piece(n).wait_recv()
        combine_flush(slice(rows_part, flush), slice(n * wide, (n + 1) * wide))
        for o in (2, 1, 3):
            give(o, n).start()
    for n in (nb,) + tuple(range(nb)):
        for o in (1, 3, 2):
            give(o, n).wait_recv()
    mine = pl.ds(pl.multiple_of(near, t_loc), t_loc)
    for h in range(2):
        y = y_acc[h, mine, :]
        for o in (1, 3, 2):
            y = y + y_recv[3 - o, h]
        y_ref[:, h * hw:(h + 1) * hw] = y.astype(y_ref.dtype)

    if b:
        @pl.loop(n_e - ring, n_e)
        def _(e):
            chunk(e).wait_send()
    for f in range(n_piece):
        for way in range(2):
            swapped(way, f).wait_send()
        if f < n_piece - 1:
            piece(f).wait_send()
    for n in range(nb + 1):
        if n < nb:
            col_piece(n).wait_send()
        for o in (1, 2, 3):
            give(o, n).wait_send()
    for c in x_own + [to_y, to_x] + to_c:
        c.wait_send()


def moe_call(b, rows_part, cols_part, fb, nb, depth, ring, out_dtype, cid, base, x, route, gates, w1, w3, w2):
    t_loc, d = x.shape
    n_e, _, f = w1.shape
    n_main = n_e * b
    flush = rows_part + cols_part
    half = 4 * t_loc
    n_piece = rows_part // fb
    dma = pltpu.SemaphoreType.DMA
    vm = pl.BlockSpec(memory_space=pltpu.VMEM)
    sm = pl.BlockSpec(memory_space=pltpu.SMEM)
    hbm = pl.BlockSpec(memory_space=pl.ANY)
    return pl.pallas_call(
        functools.partial(moe_kernel, b, rows_part, cols_part, fb, nb, depth, ring),
        out_shape=(jax.ShapeDtypeStruct((t_loc, d), out_dtype), jax.ShapeDtypeStruct((1, 1), jnp.int32)),
        in_specs=[sm, vm, vm, vm, hbm, hbm, hbm],
        out_specs=(vm, sm),
        scratch_shapes=[
            pltpu.VMEM((2 * half, d), BF16),
            pltpu.VMEM((8,) + route.shape, jnp.int32),
            pltpu.VMEM((8,) + route.shape, F32),
            pltpu.VMEM((2 * half, 2 * half), BF16),
            pltpu.VMEM((n_e, 2 * half), F32),
            pltpu.VMEM((max(n_main // 128, 1), 3, half, 128), BF16),
            pltpu.VMEM((3, half, 256), BF16),
            pltpu.VMEM((8, n_main + 256), jnp.int32),
            pltpu.SMEM((8, n_main + 256), jnp.int32),
            pltpu.VMEM((depth, d, f), BF16),
            pltpu.VMEM((depth, d, f), BF16),
            pltpu.VMEM((depth, f, d), BF16),
            pltpu.VMEM((n_e * half + 8, d), F32),
            pltpu.VMEM((ring, max(b, 8), d), F32),
            pltpu.VMEM((max(n_main, 8), d), F32),
            pltpu.VMEM((128, d), F32),
            pltpu.VMEM((2, half, d // 2), F32),
            pltpu.VMEM((3, 2, t_loc, d // 2), F32),
            pltpu.VMEM((2, 2, flush, d // 2), F32),
            pltpu.VMEM((2, flush, d // 2), F32),
            pltpu.VMEM((flush, d // 2), F32),
            pltpu.VMEM((flush, d // 2), F32),
            dma((2, 8)), dma((2, 8)), dma((11,)), dma((11,)), dma, dma((3, depth)), dma((ring,)), dma((n_e,)),
            dma((2, n_piece + 1)), dma((2, n_piece + 1)), dma((n_piece,)), dma((n_piece,)), dma((nb,)), dma((nb,)),
            dma((3, nb + 1)), dma((3, nb + 1)),
        ],
        compiler_params=pltpu.CompilerParams(collective_id=cid, has_side_effects=True, vmem_limit_bytes=67043328),
    )(base, x, route, gates, w1, w3, w2)


def solution(mesh):
    tok_spec = P(('dp', 'tp', 'ep'), None)

    def local(x, route_idx, gates, w1, w3, w2):
        zero = jnp.zeros((1,), jnp.int32)
        rt, gt = route_idx.T, gates.T
        y, need = moe_call(8, 128, 64, 32, 4, 3, 4, BF16, 1, zero, x, rt, gt, w1, w3, w2)

        def slow(_):
            part = 192

            def one(p, acc):
                base = jnp.full((1,), p * part, jnp.int32)
                return acc + moe_call(0, 128, part - 128, 32, 4, 3, 4, F32, 2, base, x, rt, gt, w1, w3, w2)[0]

            return lax.fori_loop(0, pl.cdiv(2048, part), one, jnp.zeros(x.shape, F32)).astype(BF16)

        return lax.cond(need[0, 0] > 0, slow, lambda y: y, y)

    return jax.shard_map(local, mesh=mesh,
                         in_specs=(tok_spec, tok_spec, tok_spec, P('ep', None, 'tp'), P('ep', None, 'tp'), P('ep', 'tp', None)),
                         out_specs=tok_spec, check_vma=False)
```

time: 96.2 us -> 87.3 us (0.907)
  Pallas kernels: 93.8 us -> 84.9 us
    pallas_call x1, Pallas kernels: 93.8 us -> 84.9 us  [moe_call(): pl.pallas_call(functools.partial(moe_kernel, b, rows_part, cols_part, fb,...]
where the time goes in v3:
time: 87.3 us; the launch traced here: 87.2 us
  Pallas kernels  84.9 us (97%)
  local copies, waits for them, and re-layouts  1.57 us (2%)
    pallas_call x1, Pallas kernels, moe_call(): pl.pallas_call(functools.partial(moe_kernel, b, rows_part, cols_part, fb,...  84.9 us

profile of v3, /device:TPU:0, one launch (start us, length us, event | category | flops | bytes accessed | tf_op | source)
XLA Modules:
  0.0 87.2 jit_solution(3485945047083829605)
XLA Ops:
  0.0 84.9 %shard_map.66 = (bf16[32,2048]{1,0:T(8,128)(2,1)}, s32[1,1]{1,0:T(1,128)}) custom-call(s32[1]{0:T(128)} %constant.23.clone.1.refs_0_, bf16[32,2048]{1,0:T(8,128)(2,1)} %refs_1_.1, s32[8,32]{1,0:T(8,128)} %bitcast.6, f32[8,32]{1,0:T(8,128)} %bitcast.8, bf16[32,2048,384]{2,1,0:T(8,128)(2,1)} %refs_4_.1, bf16[32,2048,384]{2,1,0:T(8,128)(2,1)} %refs_5_.1, ...), custom_call_target="tpu_custom_call" | custom-call | tf_op jit(solution)/shard_map/pallas_call | solution.py:419
  85.6 1.6 %copy.18 = bf16[32,2048]{1,0:T(8,128)(2,1)} copy(bf16[32,2048]{1,0:T(8,128)(2,1)} %get-tuple-element.159) | data formatting | bytes 262144
  (1 shorter events, 0.0 us)

commit v4 on v3

--- a/solution.py
+++ b/solution.py
@@ -29,12 +29,12 @@
     return g1, g2, g3
 
 
-def moe_kernel(b, rows_part, cols_part, fb, nb, depth, ring, *refs):
-    (base_ref, x_ref, route_ref, gates_ref, w1_ref, w3_ref, w2_ref, y_ref, need_ref,
+def moe_kernel(b, rows_part, cols_part, extra, fb, nb, depth, ring, *refs):
+    (base_ref, x_ref, route_ref, gates_ref, w1_ref, w3_ref, w2_ref, y_ref, need_ref, mb_ref, ma_ref, mg_ref,
      x_all, r_all, g_all, before, code, gm, gf, tab_v, tab_s, w1b, w3b, w2b, o_buf, send, recv, own, y_acc, y_recv,
      cand, swap, f_send, f_recv,
      gs_sem, gr_sem, xs_sem, xr_sem, tab_sem, w_sem, s_sem, r_sem, ds_sem, dr_sem, fs_sem, fr_sem, cs_sem, cr_sem,
-     ys_sem, yr_sem) = refs
+     ys_sem, yr_sem, m_sem) = refs
     tp = lax.axis_index("tp")
     ep = lax.axis_index("ep")
     t_loc, d = x_ref.shape
@@ -119,6 +119,11 @@
     for kind in range(2):
         for dt, de in others:
             gather(kind, dt, de).wait()
+
+    x_own[0].wait_recv()
+    to_y.start()
+    x_own[1].wait_recv()
+    to_x.start()
 
     route = jnp.concatenate([r_all[i] for i in range(8)], axis=1)
     gates = jnp.concatenate([g_all[i] for i in range(4)], axis=1)
@@ -142,7 +147,8 @@
     suffix = jnp.where((s_i >= k_i) & in_block, 1.0, 0.0).astype(BF16)
     left = dot(suffix, (dot(hit_all.astype(BF16), side) - b).astype(BF16))
     left = [jnp.maximum(jnp.max(left[i * n_e:(i + 1) * n_e], axis=0, keepdims=True), 0.0) for i in range(4)]
-    need_ref[0, 0] = jnp.where(jnp.max(jnp.maximum(left[0] + left[1], left[2] + left[3])) > flush, 1, 0)
+    left = jnp.max(jnp.maximum(left[0] + left[1], left[2] + left[3]))
+    need_ref[0, 0] = jnp.where(left > flush, 1, 0) + jnp.where(left > flush + extra, 1, 0)
 
     hit_b = hit.astype(BF16)
     pos = dot(hit_b, before[...])
@@ -203,10 +209,6 @@
     to_smem = pltpu.make_async_copy(tab_v, tab_s, tab_sem)
     to_smem.start()
 
-    x_own[0].wait_recv()
-    to_y.start()
-    x_own[1].wait_recv()
-    to_x.start()
     x_own[2].wait_recv()
     to_c[0].start()
     x_own[3].wait_recv()
@@ -238,8 +240,13 @@
             src_ref=send.at[slot], dst_ref=recv.at[pl.ds(pl.multiple_of(e * b, b), b)], send_sem=s_sem.at[slot],
             recv_sem=r_sem.at[e], device_id=peer, device_id_type=MESH)
 
+    n_piece = rows_part // fb + 1
+
+    def span(f):
+        return (f * fb, fb) if f < n_piece - 1 else (rows_part, cols_part) if f < n_piece else (flush, extra)
+
     def swapped(way, f):
-        rows = pl.ds(f * fb, fb) if f < rows_part // fb else pl.ds(rows_part, cols_part)
+        rows = pl.ds(*span(f))
         return pltpu.make_async_remote_copy(
             src_ref=cand.at[way, 1 - core, rows], dst_ref=swap.at[way, rows], send_sem=ds_sem.at[way, f],
             recv_sem=dr_sem.at[way, f], device_id=dev_c, device_id_type=MESH)
@@ -321,10 +328,8 @@
         pack_send(n_e - 1)
         chunk(n_e - 1).start()
 
-    n_piece = rows_part // fb + 1
-
     def pack_cand(way, f):
-        first, n = (f * fb, fb) if f < n_piece - 1 else (rows_part, cols_part)
+        first, n = span(f)
 
         @pl.loop(0, n // 8)
         def _(g):
@@ -344,6 +349,11 @@
         else:
             for n in range(nb):
                 col_piece(n).start()
+
+    def more():
+        return [pltpu.make_async_copy(f_send.at[pl.ds(flush, extra)], mb_ref, m_sem.at[0]),
+                pltpu.make_async_copy(swap.at[0, pl.ds(flush, extra)], ma_ref, m_sem.at[1]),
+                pltpu.make_async_copy(gf, mg_ref, m_sem.at[2])]
 
     def give(o, n):
         to = lax.rem(ep + o, 4)
@@ -367,8 +377,19 @@
         give(o, nb).start()
     for f in range(n_piece):
         pack_cand(0, f)
+    if extra:
+        pack_cand(1, n_piece)
+        pack_cand(0, n_piece)
     for f in range(n_piece):
         swapped(0, f).wait_recv()
+    if extra:
+        rows = slice(flush, flush + extra)
+        for way in range(2):
+            swapped(way, n_piece).wait_recv()
+        f_send[rows, :] = cand[1, core, rows, :] + swap[1, rows, :]
+        swap[0, rows, :] = cand[0, core, rows, :] + swap[0, rows, :]
+        for c in more():
+            c.start()
     for f in range(n_piece - 1):
         piece(f).wait_recv()
     combine_flush(slice(0, rows_part), slice(0, hw))
@@ -391,6 +412,11 @@
         @pl.loop(n_e - ring, n_e)
         def _(e):
             chunk(e).wait_send()
+    if extra:
+        for way in range(2):
+            swapped(way, n_piece).wait_send()
+        for c in more():
+            c.wait()
     for f in range(n_piece):
         for way in range(2):
             swapped(way, f).wait_send()
@@ -405,7 +431,7 @@
         c.wait_send()
 
 
-def moe_call(b, rows_part, cols_part, fb, nb, depth, ring, out_dtype, cid, base, x, route, gates, w1, w3, w2):
+def moe_call(b, rows_part, cols_part, extra, fb, nb, depth, ring, cid, base, x, route, gates, w1, w3, w2):
     t_loc, d = x.shape
     n_e, _, f = w1.shape
     n_main = n_e * b
@@ -417,10 +443,12 @@
     sm = pl.BlockSpec(memory_space=pltpu.SMEM)
     hbm = pl.BlockSpec(memory_space=pl.ANY)
     return pl.pallas_call(
-        functools.partial(moe_kernel, b, rows_part, cols_part, fb, nb, depth, ring),
-        out_shape=(jax.ShapeDtypeStruct((t_loc, d), out_dtype), jax.ShapeDtypeStruct((1, 1), jnp.int32)),
+        functools.partial(moe_kernel, b, rows_part, cols_part, extra, fb, nb, depth, ring),
+        out_shape=(jax.ShapeDtypeStruct((t_loc, d), F32), jax.ShapeDtypeStruct((1, 1), jnp.int32),
+                   jax.ShapeDtypeStruct((max(extra, 8), d // 2), F32), jax.ShapeDtypeStruct((max(extra, 8), d // 2), F32),
+                   jax.ShapeDtypeStruct((3, half, 256), BF16)),
         in_specs=[sm, vm, vm, vm, hbm, hbm, hbm],
-        out_specs=(vm, sm),
+        out_specs=(vm, sm, hbm, hbm, hbm),
         scratch_shapes=[
             pltpu.VMEM((2 * half, d), BF16),
             pltpu.VMEM((8,) + route.shape, jnp.int32),
@@ -440,36 +468,107 @@
             pltpu.VMEM((128, d), F32),
             pltpu.VMEM((2, half, d // 2), F32),
             pltpu.VMEM((3, 2, t_loc, d // 2), F32),
-            pltpu.VMEM((2, 2, flush, d // 2), F32),
-            pltpu.VMEM((2, flush, d // 2), F32),
-            pltpu.VMEM((flush, d // 2), F32),
+            pltpu.VMEM((2, 2, flush + extra, d // 2), F32),
+            pltpu.VMEM((2, flush + extra, d // 2), F32),
+            pltpu.VMEM((flush + extra, d // 2), F32),
             pltpu.VMEM((flush, d // 2), F32),
             dma((2, 8)), dma((2, 8)), dma((11,)), dma((11,)), dma, dma((3, depth)), dma((ring,)), dma((n_e,)),
-            dma((2, n_piece + 1)), dma((2, n_piece + 1)), dma((n_piece,)), dma((n_piece,)), dma((nb,)), dma((nb,)),
-            dma((3, nb + 1)), dma((3, nb + 1)),
+            dma((2, n_piece + 2)), dma((2, n_piece + 2)), dma((n_piece,)), dma((n_piece,)), dma((nb,)), dma((nb,)),
+            dma((3, nb + 1)), dma((3, nb + 1)), dma((3,)),
         ],
         compiler_params=pltpu.CompilerParams(collective_id=cid, has_side_effects=True, vmem_limit_bytes=67043328),
     )(base, x, route, gates, w1, w3, w2)
 
 
+def more_kernel(first, n_piece, y1_ref, mb_ref, ma_ref, mg_ref, y_ref, recv, acc, y2, y_recv, s_sem, r_sem, ys_sem, yr_sem):
+    tp = lax.axis_index("tp")
+    ep = lax.axis_index("ep")
+    core = lax.rem(ep, 2)
+    t_loc, d = y1_ref.shape
+    hw = d // 2
+    rows, wide = mb_ref.shape[0], hw // n_piece
+    peer = {"tp": lax.rem(tp + 1, 2), "ep": ep}
+    mates = [{"tp": tp, "ep": lax.rem(ep + o, 4)} for o in (1, 2, 3)]
+    barrier = pltpu.get_barrier_semaphore()
+    for to in [peer] + mates:
+        pl.semaphore_signal(barrier, inc=1, device_id=to, device_id_type=MESH)
+    pl.semaphore_wait(barrier, 4)
+
+    def piece(n):
+        cols = pl.ds(n * wide, wide)
+        return pltpu.make_async_remote_copy(src_ref=mb_ref.at[:, cols], dst_ref=recv.at[:, cols], send_sem=s_sem.at[n],
+                                            recv_sem=r_sem.at[n], device_id=peer, device_id_type=MESH)
+
+    def give(o, n):
+        to = lax.rem(ep + o, 4)
+        cols = pl.ds(n * wide, wide)
+        return pltpu.make_async_remote_copy(
+            src_ref=acc.at[pl.ds(pl.multiple_of(to * t_loc, t_loc), t_loc), cols], dst_ref=y_recv.at[3 - o, :, cols],
+            send_sem=ys_sem.at[o - 1, n], recv_sem=yr_sem.at[3 - o, n], device_id=mates[o - 1], device_id_type=MESH)
+
+    for n in range(n_piece):
+        piece(n).start()
+    for n in range(n_piece):
+        cols = slice(n * wide, (n + 1) * wide)
+        piece(n).wait_recv()
+        o = (recv[:, cols] + ma_ref[:, cols]).astype(BF16)
+        acc[:, cols] = sum(dot(mg_ref[j, :, first:first + rows], o) for j in range(3))
+        for o in (2, 1, 3):
+            give(o, n).start()
+    for h in range(2):
+        y2[h] = y1_ref[:, h * hw:(h + 1) * hw]
+    for n in range(n_piece):
+        for o in (1, 2, 3):
+            give(o, n).wait_recv()
+    y2[core] += acc[pl.ds(pl.multiple_of(ep * t_loc, t_loc), t_loc), :] + y_recv[1]
+    y2[1 - core] += y_recv[0] + y_recv[2]
+    for h in range(2):
+        y_ref[:, h * hw:(h + 1) * hw] = y2[h]
+    for n in range(n_piece):
+        piece(n).wait_send()
+        for o in (1, 2, 3):
+            give(o, n).wait_send()
+
+
+def more_call(first, n_piece, cid, y1, mb, ma, mg):
+    t_loc, d = y1.shape
+    dma = pltpu.SemaphoreType.DMA
+    vm = pl.BlockSpec(memory_space=pltpu.VMEM)
+    return pl.pallas_call(
+        functools.partial(more_kernel, first, n_piece),
+        out_shape=jax.ShapeDtypeStruct((t_loc, d), F32),
+        in_specs=[vm] * 4,
+        out_specs=vm,
+        scratch_shapes=[
+            pltpu.VMEM(mb.shape, F32),
+            pltpu.VMEM((4 * t_loc, d // 2), F32),
+            pltpu.VMEM((2, t_loc, d // 2), F32),
+            pltpu.VMEM((3, t_loc, d // 2), F32),
+            dma((n_piece,)), dma((n_piece,)), dma((3, n_piece)), dma((3, n_piece)),
+        ],
+        compiler_params=pltpu.CompilerParams(collective_id=cid, has_side_effects=True, vmem_limit_bytes=32000000),
+    )(y1, mb, ma, mg)
+
+
 def solution(mesh):
     tok_spec = P(('dp', 'tp', 'ep'), None)
 
     def local(x, route_idx, gates, w1, w3, w2):
+        rt, gt = route_idx.T, gates.T
         zero = jnp.zeros((1,), jnp.int32)
-        rt, gt = route_idx.T, gates.T
-        y, need = moe_call(8, 128, 64, 32, 4, 3, 4, BF16, 1, zero, x, rt, gt, w1, w3, w2)
-
-        def slow(_):
+        y1, need, mb, ma, mg = moe_call(8, 80, 64, 96, 16, 8, 3, 4, 1, zero, x, rt, gt, w1, w3, w2)
+
+        def slow(y1, mb, ma, mg):
             part = 192
 
             def one(p, acc):
                 base = jnp.full((1,), p * part, jnp.int32)
-                return acc + moe_call(0, 128, part - 128, 32, 4, 3, 4, F32, 2, base, x, rt, gt, w1, w3, w2)[0]
-
-            return lax.fori_loop(0, pl.cdiv(2048, part), one, jnp.zeros(x.shape, F32)).astype(BF16)
-
-        return lax.cond(need[0, 0] > 0, slow, lambda y: y, y)
+                return acc + moe_call(0, part - 64, 64, 0, 32, 8, 3, 4, 2, base, x, rt, gt, w1, w3, w2)[0]
+
+            return lax.fori_loop(0, pl.cdiv(2048, part), one, jnp.zeros(x.shape, F32))
+
+        y = lax.switch(need[0, 0], [lambda y1, mb, ma, mg: y1, functools.partial(more_call, 144, 4, 3), slow], y1, mb, ma, mg)
+        return y.astype(BF16)
 
     return jax.shard_map(local, mesh=mesh,
                          in_specs=(tok_spec, tok_spec, tok_spec, P('ep', None, 'tp'), P('ep', None, 'tp'), P('ep', 'tp', None)),

time: 87.3 us -> 82.9 us (0.950)
  Pallas kernels: 84.9 us -> 80.5 us
  other arithmetic: 0 us -> 1.62 us
  local copies, waits for them, and re-layouts: 1.57 us -> 0 us
    pallas_call x1, Pallas kernels: 84.9 us -> 80.5 us  [moe_call(): pl.pallas_call(functools.partial(moe_kernel, b, rows_part, cols_part, ext...]
    convert_element_type x0 -> x1, other arithmetic: none -> 1.62 us  [local(): return y.astype(BF16)]
    unnamed x1 -> x0, local copies, waits for them, and re-layouts: 1.57 us -> none
where the time goes in v4:
time: 82.9 us; the launch traced here: 82.7 us
  Pallas kernels  80.5 us (97%)
  other arithmetic  1.62 us (2%)
    pallas_call x1, Pallas kernels, moe_call(): pl.pallas_call(functools.partial(moe_kernel, b, rows_part, cols_part, ext...  80.5 us

profile of v4, /device:TPU:0, one launch (start us, length us, event | category | flops | bytes accessed | tf_op | source)
XLA Modules:
  0.0 82.7 jit_solution(17466332967902289268)
XLA Ops:
  0.0 80.5 %shard_map.64 = (f32[32,2048]{1,0:T(8,128)}, s32[1,1]{1,0:T(1,128)}, f32[96,1024]{1,0:T(8,128)}, f32[96,1024]{1,0:T(8,128)}, bf16[3,128,256]{2,1,0:T(8,128)(2,1)}) custom-call(s32[1]{0:T(128)} %constant.26.clone.1.refs_0_, bf16[32,2048]{1,0:T(8,128)(2,1)} %refs_1_.1, s32[8,32]{1,0:T(8,128)} %bitcast.6, f32[8,32]{1,0:T(8,128)} %bitcast.8, ...), custom_call_target="tpu_custom_call" | custom-call | tf_op jit(solution)/shard_map/pallas_call | solution.py:445
  81.1 1.6 %convert_element_type.11 = bf16[32,2048]{1,0:T(8,128)(2,1)} convert(f32[32,2048]{1,0:T(8,128)} %get-tuple-element.314) | non-fusion elementwise | flops 65536 | bytes 393216 | tf_op jit(solution)/shard_map/convert_element_type | solution.py:571
  (1 shorter events, 0.0 us)

commit v5 on v4

--- a/solution.py
+++ b/solution.py
@@ -33,7 +33,7 @@
     (base_ref, x_ref, route_ref, gates_ref, w1_ref, w3_ref, w2_ref, y_ref, need_ref, mb_ref, ma_ref, mg_ref,
      x_all, r_all, g_all, before, code, gm, gf, tab_v, tab_s, w1b, w3b, w2b, o_buf, send, recv, own, y_acc, y_recv,
      cand, swap, f_send, f_recv,
-     gs_sem, gr_sem, xs_sem, xr_sem, tab_sem, w_sem, s_sem, r_sem, ds_sem, dr_sem, fs_sem, fr_sem, cs_sem, cr_sem,
+     i_sem, gs_sem, gr_sem, xs_sem, xr_sem, tab_sem, w_sem, s_sem, r_sem, ds_sem, dr_sem, fs_sem, fr_sem, cs_sem, cr_sem,
      ys_sem, yr_sem, m_sem) = refs
     tp = lax.axis_index("tp")
     ep = lax.axis_index("ep")
@@ -60,29 +60,37 @@
                 pltpu.make_async_copy(w3_ref.at[e], w3b.at[slot], w_sem.at[1, slot]),
                 pltpu.make_async_copy(w2_ref.at[e], w2b.at[slot], w_sem.at[2, slot])]
 
-    for e in range(depth):
-        for c in weights(e, e):
-            c.start()
-
     others = [(dt, de) for dt in range(2) for de in range(4) if (dt, de) != (0, 0)]
 
     def device(dt, de):
         return {"tp": lax.rem(tp + dt, 2), "ep": lax.rem(ep + de, 4)}
+
 
     barrier = pltpu.get_barrier_semaphore()
     for dt, de in others:
         pl.semaphore_signal(barrier, inc=1, device_id=device(dt, de), device_id_type=MESH)
 
+    mine = pl.ds(pl.multiple_of(ep * t_loc, t_loc), t_loc)
+    inputs = [pltpu.make_async_copy(route_ref, r_all.at[ep], i_sem.at[0]),
+              pltpu.make_async_copy(gates_ref, g_all.at[ep], i_sem.at[1]),
+              pltpu.make_async_copy(x_ref, x_all.at[mine], i_sem.at[2])]
+    for c in inputs:
+        c.start()
     t_i, u_i = iota((n_tok, n_tok), 0), iota((n_tok, n_tok), 1)
     before[...] = jnp.where((t_i < u_i) & ((t_i < half) == (u_i < half)), 1.0, 0.0).astype(BF16)
     y_acc[...] = jnp.zeros_like(y_acc)
     o_buf[n_e * half:, :] = jnp.zeros((8, d), F32)
+    for c in inputs:
+        c.wait()
+    for e in range(depth):
+        for c in weights(e, e):
+            c.start()
     pl.semaphore_wait(barrier, len(others))
 
     def gather(kind, dt, de):
-        src, dst = ((route_ref, r_all), (gates_ref, g_all))[kind]
+        dst = (r_all, g_all)[kind]
         return pltpu.make_async_remote_copy(
-            src_ref=src, dst_ref=dst.at[dt * 4 + ep], send_sem=gs_sem.at[kind, dt * 4 + de],
+            src_ref=dst.at[ep], dst_ref=dst.at[dt * 4 + ep], send_sem=gs_sem.at[kind, dt * 4 + de],
             recv_sem=gr_sem.at[kind, dt * 4 + de], device_id=device(dt, de), device_id_type=MESH)
 
     def rows_of(first, n):
@@ -94,11 +102,11 @@
 
     near, far, h_loc = ep * t_loc, half + ep * t_loc, t_loc // 2
     nx = ep_x * t_loc
-    x_own = [x_copy(0, x_ref.at[pl.ds(0, h_loc)], rows_of(near, h_loc), dev_x),
-             x_copy(1, x_ref.at[pl.ds(h_loc, h_loc)], rows_of(far + h_loc, h_loc), peer),
-             x_copy(2, x_ref.at[pl.ds(h_loc, h_loc)], rows_of(near + h_loc, h_loc), dev_x),
-             x_copy(3, x_ref.at[pl.ds(0, h_loc)], rows_of(far, h_loc), peer),
-             x_copy(4, x_ref, rows_of(near, t_loc), dev_c)]
+    x_own = [x_copy(0, rows_of(near, h_loc), rows_of(near, h_loc), dev_x),
+             x_copy(1, rows_of(near + h_loc, h_loc), rows_of(far + h_loc, h_loc), peer),
+             x_copy(2, rows_of(near + h_loc, h_loc), rows_of(near + h_loc, h_loc), dev_x),
+             x_copy(3, rows_of(near, h_loc), rows_of(far, h_loc), peer),
+             x_copy(4, rows_of(near, t_loc), rows_of(near, t_loc), dev_c)]
 
     def passed(i, row, n, to):
         return x_copy(i, rows_of(row, n), rows_of(row, n), to)
@@ -113,9 +121,6 @@
             gather(kind, dt, de).start()
     for c in x_own:
         c.start()
-    r_all[ep] = route_ref[...]
-    g_all[ep] = gates_ref[...]
-    x_all[pl.ds(pl.multiple_of(near, t_loc), t_loc), :] = x_ref[...]
     for kind in range(2):
         for dt, de in others:
             gather(kind, dt, de).wait()
@@ -401,7 +406,6 @@
     for n in (nb,) + tuple(range(nb)):
         for o in (1, 3, 2):
             give(o, n).wait_recv()
-    mine = pl.ds(pl.multiple_of(near, t_loc), t_loc)
     for h in range(2):
         y = y_acc[h, mine, :]
         for o in (1, 3, 2):
@@ -447,7 +451,7 @@
         out_shape=(jax.ShapeDtypeStruct((t_loc, d), F32), jax.ShapeDtypeStruct((1, 1), jnp.int32),
                    jax.ShapeDtypeStruct((max(extra, 8), d // 2), F32), jax.ShapeDtypeStruct((max(extra, 8), d // 2), F32),
                    jax.ShapeDtypeStruct((3, half, 256), BF16)),
-        in_specs=[sm, vm, vm, vm, hbm, hbm, hbm],
+        in_specs=[sm, hbm, hbm, hbm, hbm, hbm, hbm],
         out_specs=(vm, sm, hbm, hbm, hbm),
         scratch_shapes=[
             pltpu.VMEM((2 * half, d), BF16),
@@ -472,7 +476,7 @@
             pltpu.VMEM((2, flush + extra, d // 2), F32),
             pltpu.VMEM((flush + extra, d // 2), F32),
             pltpu.VMEM((flush, d // 2), F32),
-            dma((2, 8)), dma((2, 8)), dma((11,)), dma((11,)), dma, dma((3, depth)), dma((ring,)), dma((n_e,)),
+            dma((3,)), dma((2, 8)), dma((2, 8)), dma((11,)), dma((11,)), dma, dma((3, depth)), dma((ring,)), dma((n_e,)),
             dma((2, n_piece + 2)), dma((2, n_piece + 2)), dma((n_piece,)), dma((n_piece,)), dma((nb,)), dma((nb,)),
             dma((3, nb + 1)), dma((3, nb + 1)), dma((3,)),
         ],

time: 82.9 us -> 82 us (0.989)
  Pallas kernels: 80.5 us -> 79.6 us
    pallas_call x1, Pallas kernels: 80.5 us -> 79.6 us  [moe_call(): pl.pallas_call(functools.partial(moe_kernel, b, rows_part, cols_part, ext...]
where the time goes in v5:
time: 82 us; the launch traced here: 81.8 us
  Pallas kernels  79.6 us (97%)
  other arithmetic  1.62 us (2%)
    pallas_call x1, Pallas kernels, moe_call(): pl.pallas_call(functools.partial(moe_kernel, b, rows_part, cols_part, ext...  79.6 us

profile of v5, /device:TPU:0, one launch (start us, length us, event | category | flops | bytes accessed | tf_op | source)
XLA Modules:
  0.0 81.8 jit_solution(171646600610164684)
XLA Ops:
  0.0 79.6 %shard_map.64 = (f32[32,2048]{1,0:T(8,128)}, s32[1,1]{1,0:T(1,128)}, f32[96,1024]{1,0:T(8,128)}, f32[96,1024]{1,0:T(8,128)}, bf16[3,128,256]{2,1,0:T(8,128)(2,1)}) custom-call(s32[1]{0:T(128)} %constant.26.clone.1.refs_0_, bf16[32,2048]{1,0:T(8,128)(2,1)} %refs_1_.1, s32[8,32]{1,0:T(8,128)} %bitcast.6, f32[8,32]{1,0:T(8,128)} %bitcast.8, ...), custom_call_target="tpu_custom_call" | custom-call | tf_op jit(solution)/shard_map/pallas_call | solution.py:449
  80.2 1.6 %convert_element_type.11 = bf16[32,2048]{1,0:T(8,128)(2,1)} convert(f32[32,2048]{1,0:T(8,128)} %get-tuple-element.314) | non-fusion elementwise | flops 65536 | bytes 393216 | tf_op jit(solution)/shard_map/convert_element_type | solution.py:575
  (1 shorter events, 0.0 us)

commit v6 on v5

--- a/solution.py
+++ b/solution.py
@@ -29,7 +29,11 @@
     return g1, g2, g3
 
 
-def moe_kernel(b, rows_part, cols_part, extra, fb, nb, depth, ring, *refs):
+def chunk_of(k, skip):
+    return k - lax.div(k, skip)
+
+
+def moe_kernel(skip, b, rows_part, cols_part, some, extra, fb, nb, depth, ring, *refs):
     (base_ref, x_ref, route_ref, gates_ref, w1_ref, w3_ref, w2_ref, y_ref, need_ref, mb_ref, ma_ref, mg_ref,
      x_all, r_all, g_all, before, code, gm, gf, tab_v, tab_s, w1b, w3b, w2b, o_buf, send, recv, own, y_acc, y_recv,
      cand, swap, f_send, f_recv,
@@ -42,8 +46,8 @@
     half = 4 * t_loc
     n_tok = 2 * half
     flush = rows_part + cols_part
-    n_main = n_e * b
-    lag = 4
+    n_chunk = n_e - (n_e - 1) // skip
+    n_main = pl.cdiv(n_chunk * b, 128) * 128
     hw = d // 2
     wide = hw // nb
     core = lax.rem(ep, 2)
@@ -80,6 +84,8 @@
     before[...] = jnp.where((t_i < u_i) & ((t_i < half) == (u_i < half)), 1.0, 0.0).astype(BF16)
     y_acc[...] = jnp.zeros_like(y_acc)
     o_buf[n_e * half:, :] = jnp.zeros((8, d), F32)
+    if n_main > n_chunk * b:
+        recv[n_chunk * b:, :] = jnp.zeros((n_main - n_chunk * b, d), F32)
     for c in inputs:
         c.wait()
     for e in range(depth):
@@ -150,10 +156,13 @@
     k_i, s_i = iota((n_all, n_all), 0), iota((n_all, n_all), 1)
     in_block = functools.reduce(lambda a, c: a | c, [(k_i >= i * n_e) & (k_i < (i + 1) * n_e) & (s_i >= i * n_e) & (s_i < (i + 1) * n_e) for i in range(4)])
     suffix = jnp.where((s_i >= k_i) & in_block, 1.0, 0.0).astype(BF16)
-    left = dot(suffix, (dot(hit_all.astype(BF16), side) - b).astype(BF16))
+    at = iota((n_all, 128), 0).astype(F32)
+    at = at - n_e * jnp.floor((at + 0.5) * (1.0 / n_e))
+    sends = jnp.where((at > 0) & (at == skip * jnp.floor((at + 0.5) * (1.0 / skip))), 0.0, float(b))
+    left = dot(suffix, (dot(hit_all.astype(BF16), side) - sends).astype(BF16))
     left = [jnp.maximum(jnp.max(left[i * n_e:(i + 1) * n_e], axis=0, keepdims=True), 0.0) for i in range(4)]
     left = jnp.max(jnp.maximum(left[0] + left[1], left[2] + left[3]))
-    need_ref[0, 0] = jnp.where(left > flush, 1, 0) + jnp.where(left > flush + extra, 1, 0)
+    need_ref[0, 0] = sum(jnp.where(left > flush + m, 1, 0) for m in (0, some, extra))
 
     hit_b = hit.astype(BF16)
     pos = dot(hit_b, before[...])
@@ -164,6 +173,7 @@
     cum = dot(upto, dot(hit_b, side).astype(BF16))
 
     def served(c, m, k_f):
+        k_f = k_f - jnp.floor((k_f + 0.5) * (1.0 / skip))
         inner = jnp.min(jnp.where(k_f <= m, c + b * (m - k_f), BIG), axis=0, keepdims=True)
         return jnp.minimum(inner, b * (m + 1.0))
 
@@ -180,7 +190,7 @@
         i_f = iota((1, n_main), 1).astype(F32)
         step = jnp.floor((i_f + 0.5) * (1.0 / b))
         q = served(c, step - 1.0, k_f) + (i_f - step * b)
-        valid = q < served(c, step, k_f)
+        valid = (q < served(c, step, k_f)) & (step < n_chunk)
         return locate(c, q, valid, shift) + (valid,)
 
     def flush_table(way, shift):
@@ -188,7 +198,7 @@
         i_f = iota((1, 256), 1).astype(F32) + base_ref[0].astype(F32)
         both = []
         for c in (cum[:n_e, way:way + 1], cum[n_e:, way:way + 1]):
-            done = served(c, float(n_e - 1), k_f)
+            done = served(c, float(n_chunk - 1), k_f)
             both.append((c, done, jnp.max(c, axis=0, keepdims=True) - done))
         second = core.astype(F32)
         out = []
@@ -280,7 +290,7 @@
             own[pl.ds(first + r, 1), :] = partial(1, e * b + r)
 
     def combine_main(m):
-        @pl.loop(m * (128 // b), (m + 1) * (128 // b))
+        @pl.loop(m * (128 // b), min((m + 1) * (128 // b), n_chunk))
         def _(e):
             chunk(e).wait_recv()
         for h in range(2):
@@ -298,18 +308,17 @@
     def _(e):
         slot = lax.rem(e, depth)
         if b:
-            @pl.when(e > ring)
+            @pl.when((e == 1) | ((e > 1) & (lax.rem(e - 1, skip) != 0)))
             def _():
-                chunk(e - 1 - ring).wait_send()
-
-            @pl.when(e >= 1)
-            def _():
-                pack_send(e - 1)
-                chunk(e - 1).start()
+                c = chunk_of(e - 1, skip)
+
+                @pl.when(c >= ring)
+                def _():
+                    chunk(c - ring).wait_send()
+                pack_send(c)
+                chunk(c).start()
         for c in weights(e, slot):
             c.wait()
-        if b:
-            pack_own(jnp.maximum(e - lag, 0))
         pick = jnp.where(code[pl.ds(e, 1), :] == slot_i, 1.0, 0.0).astype(BF16)
         xs = dot(pick, x_all[...]).astype(BF16)
         u = dot(xs, w1b[slot])
@@ -322,16 +331,10 @@
             for c in weights(e + depth, slot):
                 c.start()
 
-        if b:
-            for m in range(n_main // 128 - 1):
-                @pl.when(e == (m + 1) * 128 // b - 1 + lag)
-                def _():
-                    combine_main(m)
-
     if b:
-        chunk(n_e - 1 - ring).wait_send()
-        pack_send(n_e - 1)
-        chunk(n_e - 1).start()
+        chunk(n_chunk - 1 - ring).wait_send()
+        pack_send(n_chunk - 1)
+        chunk(n_chunk - 1).start()
 
     def pack_cand(way, f):
         first, n = span(f)
@@ -373,11 +376,11 @@
         join_send(f)
         if f + 2 < n_piece:
             pack_cand(1, f + 2)
-    if b:
-        @pl.loop(n_e - lag, n_e)
-        def _(e):
-            pack_own(e)
-        combine_main(n_main // 128 - 1)
+    for m in range(n_main // 128):
+        @pl.loop(m * (128 // b), min((m + 1) * (128 // b), n_chunk))
+        def _(c):
+            pack_own(c)
+        combine_main(m)
     for o in (2, 1, 3):
         give(o, nb).start()
     for f in range(n_piece):
@@ -413,7 +416,7 @@
         y_ref[:, h * hw:(h + 1) * hw] = y.astype(y_ref.dtype)
 
     if b:
-        @pl.loop(n_e - ring, n_e)
+        @pl.loop(n_chunk - ring, n_chunk)
         def _(e):
             chunk(e).wait_send()
     if extra:
@@ -435,10 +438,10 @@
         c.wait_send()
 
 
-def moe_call(b, rows_part, cols_part, extra, fb, nb, depth, ring, cid, base, x, route, gates, w1, w3, w2):
+def moe_call(skip, b, rows_part, cols_part, some, extra, fb, nb, depth, ring, cid, base, x, route, gates, w1, w3, w2):
     t_loc, d = x.shape
     n_e, _, f = w1.shape
-    n_main = n_e * b
+    n_main = pl.cdiv((n_e - (n_e - 1) // skip) * b, 128) * 128
     flush = rows_part + cols_part
     half = 4 * t_loc
     n_piece = rows_part // fb
@@ -447,7 +450,7 @@
     sm = pl.BlockSpec(memory_space=pltpu.SMEM)
     hbm = pl.BlockSpec(memory_space=pl.ANY)
     return pl.pallas_call(
-        functools.partial(moe_kernel, b, rows_part, cols_part, extra, fb, nb, depth, ring),
+        functools.partial(moe_kernel, skip, b, rows_part, cols_part, some, extra, fb, nb, depth, ring),
         out_shape=(jax.ShapeDtypeStruct((t_loc, d), F32), jax.ShapeDtypeStruct((1, 1), jnp.int32),
                    jax.ShapeDtypeStruct((max(extra, 8), d // 2), F32), jax.ShapeDtypeStruct((max(extra, 8), d // 2), F32),
                    jax.ShapeDtypeStruct((3, half, 256), BF16)),
@@ -484,13 +487,13 @@
     )(base, x, route, gates, w1, w3, w2)
 
 
-def more_kernel(first, n_piece, y1_ref, mb_ref, ma_ref, mg_ref, y_ref, recv, acc, y2, y_recv, s_sem, r_sem, ys_sem, yr_sem):
+def more_kernel(first, rows, n_piece, y1_ref, mb_ref, ma_ref, mg_ref, y_ref, recv, acc, y2, y_recv, s_sem, r_sem, ys_sem, yr_sem):
     tp = lax.axis_index("tp")
     ep = lax.axis_index("ep")
     core = lax.rem(ep, 2)
     t_loc, d = y1_ref.shape
     hw = d // 2
-    rows, wide = mb_ref.shape[0], hw // n_piece
+    wide = hw // n_piece
     peer = {"tp": lax.rem(tp + 1, 2), "ep": ep}
     mates = [{"tp": tp, "ep": lax.rem(ep + o, 4)} for o in (1, 2, 3)]
     barrier = pltpu.get_barrier_semaphore()
@@ -500,7 +503,7 @@
 
     def piece(n):
         cols = pl.ds(n * wide, wide)
-        return pltpu.make_async_remote_copy(src_ref=mb_ref.at[:, cols], dst_ref=recv.at[:, cols], send_sem=s_sem.at[n],
+        return pltpu.make_async_remote_copy(src_ref=mb_ref.at[pl.ds(0, rows), cols], dst_ref=recv.at[:, cols], send_sem=s_sem.at[n],
                                             recv_sem=r_sem.at[n], device_id=peer, device_id_type=MESH)
 
     def give(o, n):
@@ -515,7 +518,7 @@
     for n in range(n_piece):
         cols = slice(n * wide, (n + 1) * wide)
         piece(n).wait_recv()
-        o = (recv[:, cols] + ma_ref[:, cols]).astype(BF16)
+        o = (recv[:, cols] + ma_ref[:rows, cols]).astype(BF16)
         acc[:, cols] = sum(dot(mg_ref[j, :, first:first + rows], o) for j in range(3))
         for o in (2, 1, 3):
             give(o, n).start()
@@ -534,17 +537,17 @@
             give(o, n).wait_send()
 
 
-def more_call(first, n_piece, cid, y1, mb, ma, mg):
+def more_call(first, rows, n_piece, cid, y1, mb, ma, mg):
     t_loc, d = y1.shape
     dma = pltpu.SemaphoreType.DMA
     vm = pl.BlockSpec(memory_space=pltpu.VMEM)
     return pl.pallas_call(
-        functools.partial(more_kernel, first, n_piece),
+        functools.partial(more_kernel, first, rows, n_piece),
         out_shape=jax.ShapeDtypeStruct((t_loc, d), F32),
         in_specs=[vm] * 4,
         out_specs=vm,
         scratch_shapes=[
-            pltpu.VMEM(mb.shape, F32),
+            pltpu.VMEM((rows, d // 2), F32),
             pltpu.VMEM((4 * t_loc, d // 2), F32),
             pltpu.VMEM((2, t_loc, d // 2), F32),
             pltpu.VMEM((3, t_loc, d // 2), F32),
@@ -560,18 +563,18 @@
     def local(x, route_idx, gates, w1, w3, w2):
         rt, gt = route_idx.T, gates.T
         zero = jnp.zeros((1,), jnp.int32)
-        y1, need, mb, ma, mg = moe_call(8, 80, 64, 96, 16, 8, 3, 4, 1, zero, x, rt, gt, w1, w3, w2)
+        y1, need, mb, ma, mg = moe_call(11, 8, 96, 64, 48, 80, 16, 8, 3, 4, 1, zero, x, rt, gt, w1, w3, w2)
 
         def slow(y1, mb, ma, mg):
             part = 192
 
             def one(p, acc):
                 base = jnp.full((1,), p * part, jnp.int32)
-                return acc + moe_call(0, part - 64, 64, 0, 32, 8, 3, 4, 2, base, x, rt, gt, w1, w3, w2)[0]
+                return acc + moe_call(8, 0, part - 64, 64, 0, 0, 32, 8, 3, 4, 2, base, x, rt, gt, w1, w3, w2)[0]
 
             return lax.fori_loop(0, pl.cdiv(2048, part), one, jnp.zeros(x.shape, F32))
 
-        y = lax.switch(need[0, 0], [lambda y1, mb, ma, mg: y1, functools.partial(more_call, 144, 4, 3), slow], y1, mb, ma, mg)
+        y = lax.switch(need[0, 0], [lambda y1, mb, ma, mg: y1, functools.partial(more_call, 160, 48, 4, 3), functools.partial(more_call, 160, 80, 4, 4), slow], y1, mb, ma, mg)
         return y.astype(BF16)
 
     return jax.shard_map(local, mesh=mesh,

time: 82 us -> 81.2 us (level)
    pallas_call x1, Pallas kernels: 79.6 us -> 78.8 us  [moe_call(): pl.pallas_call(functools.partial(moe_kernel, skip, b, rows_part, cols_par...]
where the time goes in v6:
time: 81.2 us; the launch traced here: 81.1 us
  Pallas kernels  78.8 us (97%)
  other arithmetic  1.62 us (2%)
    pallas_call x1, Pallas kernels, moe_call(): pl.pallas_call(functools.partial(moe_kernel, skip, b, rows_part, cols_par...  78.8 us

profile of v6, /device:TPU:0, one launch (start us, length us, event | category | flops | bytes accessed | tf_op | source)
XLA Modules:
  0.0 81.1 jit_solution(11506364375028244661)
XLA Ops:
  0.0 78.8 %shard_map.64 = (f32[32,2048]{1,0:T(8,128)}, s32[1,1]{1,0:T(1,128)}, f32[80,1024]{1,0:T(8,128)}, f32[80,1024]{1,0:T(8,128)}, bf16[3,128,256]{2,1,0:T(8,128)(2,1)}) custom-call(s32[1]{0:T(128)} %constant.26.clone.1.refs_0_, bf16[32,2048]{1,0:T(8,128)(2,1)} %refs_1_.1, s32[8,32]{1,0:T(8,128)} %bitcast.6, f32[8,32]{1,0:T(8,128)} %bitcast.8, ...), custom_call_target="tpu_custom_call" | custom-call | tf_op jit(solution)/shard_map/pallas_call | solution.py:452
  79.5 1.6 %convert_element_type.13 = bf16[32,2048]{1,0:T(8,128)(2,1)} convert(f32[32,2048]{1,0:T(8,128)} %get-tuple-element.327) | non-fusion elementwise | flops 65536 | bytes 393216 | tf_op jit(solution)/shard_map/convert_element_type | solution.py:578
  (1 shorter events, 0.0 us)
